TPU v7x, 8 devices: a whole 2x2x1 slice. The times are simulated.
8 devices in a mesh: dp: 1 (over z), col: 2 (over y), row: 4 (over x, core).
Axes of the slice: x: 2, y: 2, z: 1, core: 2. Of those that a mesh axis runs over, the one named last changes fastest.
Arguments:
- hidden: bfloat16 [128, 2560], P('dp', 'row')
- cache_len: int32 [128], P('dp')
- k_cache: bfloat16 [2, 128, 32, 256, 80], P(None, 'dp', ('col', 'row'))
- v_cache: bfloat16 [2, 128, 32, 256, 80], P(None, 'dp', ('col', 'row'))
- ln1_g: bfloat16 [2, 2560], P(None, 'row')
- ln1_b: bfloat16 [2, 2560], P(None, 'row')
- w_q: bfloat16 [2, 2560, 2560], P(None, 'row', 'col')
- b_q: bfloat16 [2, 2560], P(None, 'col')
- w_k: bfloat16 [2, 2560, 2560], P(None, 'row', 'col')
- b_k: bfloat16 [2, 2560], P(None, 'col')
- w_v: bfloat16 [2, 2560, 2560], P(None, 'row', 'col')
- b_v: bfloat16 [2, 2560], P(None, 'col')
- w_o: bfloat16 [2, 2560, 2560], P(None, 'col', 'row')
- b_o: bfloat16 [2, 2560], P(None, 'row')
- ln2_g: bfloat16 [2, 2560], P(None, 'row')
- ln2_b: bfloat16 [2, 2560], P(None, 'row')
- w_fc1: bfloat16 [2, 2560, 10240], P(None, 'row', 'col')
- b_fc1: bfloat16 [2, 10240], P(None, 'col')
- w_fc2: bfloat16 [2, 10240, 2560], P(None, 'col', 'row')
- b_fc2: bfloat16 [2, 2560], P(None, 'row')
Outputs:
- output 1: bfloat16 [128, 2560], P('dp', 'row')
- output 2: bfloat16 [2, 128, 32, 80], P(None, 'dp', ('col', 'row'))
- output 3: bfloat16 [2, 128, 32, 80], P(None, 'dp', ('col', 'row'))
All inputs are finite; a program needn't handle non-finite values.
Results may differ from a plain program's by a relative error of at most 0.0184677.
Values are sent between devices in bfloat16 or wider.
A program may use at most 1 GiB of HBM per device.

v0:
```python
import jax
import jax.numpy as jnp
from jax import lax
from jax.sharding import PartitionSpec as P

EPS_LN = 1e-5


def attention(q_heads, k_fresh, v_fresh, k_layer, v_layer, lengths):
    scores = jnp.einsum("bhd,bhsd->bhs", q_heads, k_layer, preferred_element_type=jnp.float32)
    positions = jnp.arange(k_layer.shape[2])
    scores = jnp.where(positions[None, None, :] < lengths[:, None, None], scores, -jnp.inf)
    score_new = jnp.einsum("bhd,bhd->bh", q_heads, k_fresh, preferred_element_type=jnp.float32)
    peak = jnp.maximum(jnp.max(scores, axis=-1), score_new)
    exp_cache = jnp.exp(scores - peak[:, :, None])
    exp_new = jnp.exp(score_new - peak)
    total_mass = jnp.sum(exp_cache, axis=-1) + exp_new
    prob_cache = (exp_cache / total_mass[:, :, None]).astype(jnp.bfloat16)
    prob_new = (exp_new / total_mass).astype(jnp.bfloat16)
    mixed = jnp.einsum("bhs,bhsd->bhd", prob_cache, v_layer, preferred_element_type=jnp.float32)
    mixed = mixed + prob_new.astype(jnp.float32)[:, :, None] * v_fresh.astype(jnp.float32)
    return mixed.astype(jnp.bfloat16)


def solution(mesh):
    n_row = mesh.shape["row"]
    act_spec = P("dp", "row")
    cache_spec = P(None, "dp", ("col", "row"), None, None)
    fresh_spec = P(None, "dp", ("col", "row"), None)
    in_weight = P(None, "row", "col")
    out_weight = P(None, "col", "row")
    col_vec = P(None, "col")
    row_vec = P(None, "row")
    in_specs = (act_spec, P("dp"), cache_spec, cache_spec, row_vec, row_vec,
                in_weight, col_vec, in_weight, col_vec, in_weight, col_vec,
                out_weight, row_vec, row_vec, row_vec, in_weight, col_vec, out_weight, row_vec)

    def layer_norm(state, gain, shift):
        state_f32 = state.astype(jnp.float32)
        stats = jnp.stack([jnp.sum(state_f32, axis=-1), jnp.sum(state_f32 * state_f32, axis=-1)], axis=-1)
        stats = lax.psum(stats, "row")
        width = state.shape[-1] * n_row
        mean_val = stats[:, 0:1] / width
        variance = stats[:, 1:2] / width - mean_val * mean_val
        normed = (state_f32 - mean_val) * lax.rsqrt(variance + EPS_LN) * gain.astype(jnp.float32) + shift.astype(jnp.float32)
        return normed.astype(jnp.bfloat16)

    def head_projection(normed, weight, bias, scale):
        partial = jnp.dot(normed, weight, preferred_element_type=jnp.float32).astype(jnp.bfloat16)
        summed = lax.psum_scatter(partial, "row", scatter_dimension=1, tiled=True)
        width = summed.shape[1]
        bias_own = lax.dynamic_slice_in_dim(bias, lax.axis_index("row") * width, width)
        return ((summed.astype(jnp.float32) + bias_own.astype(jnp.float32)) * scale).astype(jnp.bfloat16)

    def local_step(hidden, cache_len, k_cache, v_cache, ln1_g, ln1_b, w_q, b_q, w_k, b_k, w_v, b_v,
                   w_o, b_o, ln2_g, ln2_b, w_fc1, b_fc1, w_fc2, b_fc2):
        batch_rows = hidden.shape[0]
        heads_dev = k_cache.shape[2]
        head_dim = k_cache.shape[4]
        scale = head_dim ** -0.5
        state = hidden
        k_rows = []
        v_rows = []
        for layer in range(w_q.shape[0]):
            normed = layer_norm(state, ln1_g[layer], ln1_b[layer])
            q_heads = head_projection(normed, w_q[layer], b_q[layer], scale).reshape(batch_rows, heads_dev, head_dim)
            k_fresh = head_projection(normed, w_k[layer], b_k[layer], 1.0).reshape(batch_rows, heads_dev, head_dim)
            v_fresh = head_projection(normed, w_v[layer], b_v[layer], 1.0).reshape(batch_rows, heads_dev, head_dim)
            attended = attention(q_heads, k_fresh, v_fresh, k_cache[layer], v_cache[layer], cache_len)
            gathered = lax.all_gather(attended.reshape(batch_rows, heads_dev * head_dim), "row", axis=1, tiled=True)
            proj_part = jnp.dot(gathered, w_o[layer], preferred_element_type=jnp.float32).astype(jnp.bfloat16)
            projected = lax.psum(proj_part, "col")
            state_mid = (state.astype(jnp.float32) + (projected.astype(jnp.float32) + b_o[layer].astype(jnp.float32))).astype(jnp.bfloat16)
            normed_two = layer_norm(state_mid, ln2_g[layer], ln2_b[layer])
            inner_part = jnp.dot(normed_two, w_fc1[layer], preferred_element_type=jnp.float32).astype(jnp.bfloat16)
            inner_sum = lax.psum(inner_part, "row")
            inner = jnp.maximum((inner_sum.astype(jnp.float32) + b_fc1[layer].astype(jnp.float32)).astype(jnp.bfloat16), 0)
            out_part = jnp.dot(inner, w_fc2[layer], preferred_element_type=jnp.float32).astype(jnp.bfloat16)
            out_sum = lax.psum(out_part, "col")
            state = (state_mid.astype(jnp.float32) + (out_sum.astype(jnp.float32) + b_fc2[layer].astype(jnp.float32))).astype(jnp.bfloat16)
            k_rows.append(k_fresh)
            v_rows.append(v_fresh)
        return state, jnp.stack(k_rows), jnp.stack(v_rows)

    return jax.shard_map(local_step, mesh=mesh, in_specs=in_specs,
                         out_specs=(act_spec, fresh_spec, fresh_spec), check_vma=False)
```

profile of v0, /device:TPU:0, one launch (start us, length us, event | category | flops | bytes accessed | tf_op | source)
XLA Modules:
  0.0 335.0 jit_solution(10201396568511078727)
XLA Ops:
  7.2 1.1 convert_reduce_fusion.3
  8.3 8.8 %psum.70 = f32[128,2]{0,1:T(2,128)S(1)} all-reduce(f32[128,2]{0,1:T(2,128)S(1)} %pad_maximum_fusion.2), channel_id=1, replica_groups=mesh['dp'=1,'col'=2,'row'=4] {'row'}, use_global_device_ids=true, to_apply=%region_2.0 | all-reduce | flops 256 | bytes 2048 | tf_op jit(solution)/shard_map/psum | solution.py:41
  17.1 0.8 convert_reduce_fusion.8
  17.9 3.1 convolution_convert_fusion.5
  21.1 3.1 convolution_convert_fusion.4
  24.3 3.0 convolution_convert_fusion.3
  27.8 8.2 %reduce-scatter.7.cloned.1.call-done = bf16[128,320]{0,1:T(8,128)(2,1)} async-done(((bf16[128,1280]{0,1:T(8,128)(2,1)}), bf16[128,320]{0,1:T(8,128)(2,1)}) %reduce-scatter.7.cloned.1.call-update) | async-done | bytes 81936 | tf_op jit(solution)/shard_map/reduce_scatter | solution.py:50
  36.0 1.0 multiply_convert_fusion.1
  37.2 16.1 %reduce-scatter.9.cloned.1.call-done = bf16[128,320]{0,1:T(8,128)(2,1)} async-done(((bf16[128,1280]{0,1:T(8,128)(2,1)}), bf16[128,320]{0,1:T(8,128)(2,1)}) %reduce-scatter.9.cloned.1.call-update) | async-done | bytes 81936 | tf_op jit(solution)/shard_map/reduce_scatter | solution.py:50
  53.3 1.0 add_convert_fusion.5
  54.3 8.4 %fusion.6 = f32[128,4,1,256]{3,2,1,0:T(1,128)S(1)} fusion(bf16[128,4,80,1]{2,3,1,0:T(2,128)(2,1)S(1)} %copy.27, bf16[2,128,4,256,80]{3,4,2,1,0:T(8,128)(2,1)} %param.22), kind=kOutput, calls=%fused_computation.6 | convolution fusion | flops 20971520 | bytes 21577728 | tf_op jit(solution)/shard_map/bhd,bhsd->bhs/dot_general | solution.py:10
  63.5 9.8 %fusion.4 = f32[128,4,1,80]{3,2,1,0:T(1,128)S(1)} fusion(bf16[2,128,4,256,80]{3,4,2,1,0:T(8,128)(2,1)} %param.23, bf16[128,4,256,1]{2,0,1,3:T(8,128)(2,1)S(1)} %fusion.102), kind=kOutput, calls=%fused_computation.4 | convolution fusion | flops 20971520 | bytes 21397504 | tf_op jit(solution)/shard_map/bhs,bhsd->bhd/dot_general | solution.py:20
  73.5 1.0 add_convert_fusion.4
  74.5 8.1 %all_gather.6 = bf16[128,1280]{0,1:T(8,128)(2,1)S(1)} all-gather(bf16[128,320]{0,1:T(8,128)(2,1)S(1)} %bitcast.148), channel_id=1, replica_groups=mesh['dp'=1,'col'=2,'row'=4] {'row'}, dimensions={1}, use_global_device_ids=true | all-gather | bytes 409600 | tf_op jit(solution)/shard_map/all_gather | solution.py:70
  82.6 2.5 fusion.64
  85.3 17.3 %all-reduce.7.cloned.1.call-done = bf16[128,640]{1,0:T(8,128)(2,1)} async-done(((bf16[128,640]{1,0:T(8,128)(2,1)}), bf16[128,640]{1,0:T(8,128)(2,1)}) %all-reduce.7.cloned.1.call-update) | async-done | bytes 163856 | tf_op jit(solution)/shard_map/psum | solution.py:72
  102.6 1.1 convert_reduce_fusion.2
  103.7 6.1 %psum.72 = f32[128,2]{0,1:T(2,128)S(1)} all-reduce(f32[128,2]{0,1:T(2,128)S(1)} %pad_maximum_fusion.3), channel_id=1, replica_groups=mesh['dp'=1,'col'=2,'row'=4] {'row'}, use_global_device_ids=true, to_apply=%region_11.12 | all-reduce | flops 256 | bytes 2048 | tf_op jit(solution)/shard_map/psum | solution.py:41
  109.8 5.2 %fusion.24 = bf16[128,5120]{1,0:T(8,128)(2,1)} fusion(bf16[2,640,5120]{2,1,0:T(8,128)(2,1)} %param.36, bf16[128,640]{1,0:T(8,128)(2,1)S(1)} %get-tuple-element.25, f32[640]{0:T(1024)S(1)} %get-tuple-element.16, f32[640]{0:T(1024)S(1)} %get-tuple-element.48, f32[128]{0:T(128)S(1)} %get-tuple-element.43, f32[128]{0:T(128)S(1)} %get-tuple-element.42), kind=kOutput, calls=%fused_computation.24 | convolution fusion | flops 840007680 | bytes 8034304 | tf_op jit(solution)/shard_map/dot_general | solution.py:75
  115.2 33.6 %all-reduce.9.cloned.1.call-done = bf16[128,5120]{1,0:T(8,128)(2,1)} async-done(((bf16[128,5120]{1,0:T(8,128)(2,1)}), bf16[128,5120]{1,0:T(8,128)(2,1)}) %all-reduce.9.cloned.1.call-update) | async-done | bytes 1310736 | tf_op jit(solution)/shard_map/psum | solution.py:76
  148.7 5.2 %fusion.54 = bf16[128,640]{1,0:T(8,128)(2,1)} fusion(bf16[2,5120,640]{2,1,0:T(8,128)(2,1)} %param.38, bf16[128,5120]{1,0:T(8,128)(2,1)} %all-reduce.9.cloned.1.call-done, f32[5120]{0:T(1024)S(1)} %bitcast.151), kind=kOutput, calls=%fused_computation.56 | convolution fusion | flops 841564160 | bytes 8048640 | tf_op jit(solution)/shard_map/dot_general | solution.py:78
  154.0 16.3 %all-reduce.11.cloned.1.call-done = bf16[128,640]{1,0:T(8,128)(2,1)} async-done(((bf16[128,640]{1,0:T(8,128)(2,1)}), bf16[128,640]{1,0:T(8,128)(2,1)}) %all-reduce.11.cloned.1.call-update) | async-done | bytes 163856 | tf_op jit(solution)/shard_map/psum | solution.py:79
  170.3 1.1 convert_reduce_fusion.1
  171.4 6.1 %psum.75 = f32[128,2]{0,1:T(2,128)S(1)} all-reduce(f32[128,2]{0,1:T(2,128)S(1)} %pad_maximum_fusion.4), channel_id=1, replica_groups=mesh['dp'=1,'col'=2,'row'=4] {'row'}, use_global_device_ids=true, to_apply=%region_16.17 | all-reduce | flops 256 | bytes 2048 | tf_op jit(solution)/shard_map/psum | solution.py:41
  177.5 3.0 convolution_convert_fusion.2
  180.7 3.0 convolution_convert_fusion.1
  184.1 3.0 convolution_convert_fusion
  187.2 8.1 %reduce-scatter.13.cloned.1.call-done = bf16[128,320]{0,1:T(8,128)(2,1)} async-done(((bf16[128,1280]{0,1:T(8,128)(2,1)}), bf16[128,320]{0,1:T(8,128)(2,1)}) %reduce-scatter.13.cloned.1.call-update) | async-done | bytes 81936 | tf_op jit(solution)/shard_map/reduce_scatter | solution.py:50
  195.3 1.0 multiply_convert_fusion
  196.5 8.4 %fusion.2 = f32[128,4,1,256]{3,2,1,0:T(1,128)S(1)} fusion(bf16[128,4,80,1]{2,3,1,0:T(2,128)(2,1)S(1)} %copy.34, bf16[2,128,4,256,80]{3,4,2,1,0:T(8,128)(2,1)} %param.22), kind=kOutput, calls=%fused_computation.2 | convolution fusion | flops 20971520 | bytes 21577728 | tf_op jit(solution)/shard_map/bhd,bhsd->bhs/dot_general | solution.py:10
  205.1 7.4 %reduce-scatter.15.cloned.1.call-done = bf16[128,320]{0,1:T(8,128)(2,1)} async-done(((bf16[128,1280]{0,1:T(8,128)(2,1)}), bf16[128,320]{0,1:T(8,128)(2,1)}) %reduce-scatter.15.cloned.1.call-update) | async-done | bytes 81936 | tf_op jit(solution)/shard_map/reduce_scatter | solution.py:50
  212.5 1.0 add_convert_fusion.3
  213.5 0.3 fusion.75
  214.1 9.8 %fusion = f32[128,4,1,80]{3,2,1,0:T(1,128)S(1)} fusion(bf16[2,128,4,256,80]{3,4,2,1,0:T(8,128)(2,1)} %param.23, bf16[128,4,256,1]{2,0,1,3:T(8,128)(2,1)S(1)} %fusion.103), kind=kOutput, calls=%fused_computation | convolution fusion | flops 20971520 | bytes 21397504 | tf_op jit(solution)/shard_map/bhs,bhsd->bhd/dot_general | solution.py:20
  224.0 5.8 %reduce-scatter.17.cloned.1.call-done = bf16[128,320]{0,1:T(8,128)(2,1)} async-done(((bf16[128,1280]{0,1:T(8,128)(2,1)}), bf16[128,320]{0,1:T(8,128)(2,1)}) %reduce-scatter.17.cloned.1.call-update) | async-done | bytes 81936 | tf_op jit(solution)/shard_map/reduce_scatter | solution.py:50
  229.7 1.0 add_convert_fusion.2
  230.8 8.1 %all_gather.7 = bf16[128,1280]{0,1:T(8,128)(2,1)S(1)} all-gather(bf16[128,320]{0,1:T(8,128)(2,1)S(1)} %bitcast.149), channel_id=1, replica_groups=mesh['dp'=1,'col'=2,'row'=4] {'row'}, dimensions={1}, use_global_device_ids=true | all-gather | bytes 409600 | tf_op jit(solution)/shard_map/all_gather | solution.py:70
  238.9 2.5 fusion.67
  241.5 17.4 %all-reduce.13.cloned.1.call-done = bf16[128,640]{1,0:T(8,128)(2,1)} async-done(((bf16[128,640]{1,0:T(8,128)(2,1)}), bf16[128,640]{1,0:T(8,128)(2,1)}) %all-reduce.13.cloned.1.call-update) | async-done | bytes 163856 | tf_op jit(solution)/shard_map/psum | solution.py:72
  258.9 1.1 convert_reduce_fusion
  260.0 6.1 %psum.77 = f32[128,2]{0,1:T(2,128)S(1)} all-reduce(f32[128,2]{0,1:T(2,128)S(1)} %pad_maximum_fusion.5), channel_id=1, replica_groups=mesh['dp'=1,'col'=2,'row'=4] {'row'}, use_global_device_ids=true, to_apply=%region_25.26 | all-reduce | flops 256 | bytes 2048 | tf_op jit(solution)/shard_map/psum | solution.py:41
  266.1 5.2 %fusion.27 = bf16[128,5120]{1,0:T(8,128)(2,1)} fusion(bf16[2,640,5120]{2,1,0:T(8,128)(2,1)} %param.36, bf16[128,640]{1,0:T(8,128)(2,1)S(1)} %get-tuple-element.23, f32[640]{0:T(1024)S(1)} %get-tuple-element.15, f32[640]{0:T(1024)S(1)} %get-tuple-element.49, f32[128]{0:T(128)S(1)} %get-tuple-element.39, f32[128]{0:T(128)S(1)} %get-tuple-element.38), kind=kOutput, calls=%fused_computation.25 | convolution fusion | flops 840007680 | bytes 8034304 | tf_op jit(solution)/shard_map/dot_general | solution.py:75
  271.4 33.6 %all-reduce.15.cloned.1.call-done = bf16[128,5120]{1,0:T(8,128)(2,1)} async-done(((bf16[128,5120]{1,0:T(8,128)(2,1)}), bf16[128,5120]{1,0:T(8,128)(2,1)}) %all-reduce.15.cloned.1.call-update) | async-done | bytes 1310736 | tf_op jit(solution)/shard_map/psum | solution.py:76
  305.0 5.1 %fusion.59 = bf16[128,640]{1,0:T(8,128)(2,1)} fusion(bf16[2,5120,640]{2,1,0:T(8,128)(2,1)} %param.38, bf16[128,5120]{1,0:T(8,128)(2,1)} %all-reduce.15.cloned.1.call-done, f32[5120]{0:T(1024)S(1)} %bitcast.150), kind=kOutput, calls=%fused_computation.57 | convolution fusion | flops 841564160 | bytes 8048640 | tf_op jit(solution)/shard_map/dot_general | solution.py:78
  310.2 0.7 pad_maximum_fusion
  310.9 0.7 pad_maximum_fusion.1
  311.5 15.0 %all-reduce.17.cloned.1.call-done = bf16[128,640]{1,0:T(8,128)(2,1)} async-done(((bf16[128,640]{1,0:T(8,128)(2,1)}), bf16[128,640]{1,0:T(8,128)(2,1)}) %all-reduce.17.cloned.1.call-update) | async-done | bytes 163856 | tf_op jit(solution)/shard_map/psum | solution.py:79
  326.5 1.6 fusion.101
  (84 shorter events, 3.7 us)
Async XLA Ops:
  7.2 17.1 %copy-start = (bf16[128,640]{1,0:T(8,128)(2,1)S(1)}, bf16[128,640]{1,0:T(8,128)(2,1)}, u32[]{:S(2)}) copy-start(bf16[128,640]{1,0:T(8,128)(2,1)} %param.20) | copy-start | bytes 491524
  7.2 28.9 %reduce-scatter.7.cloned.1.call-start = ((), (), s32[]{:S(2)}) async-start(), calls=%async_computation.6 | async-start | bytes 409600 | tf_op jit(solution)/shard_map/reduce_scatter | solution.py:50
  21.0 6.4 %copy-start.2 = (bf16[2,1280]{1,0:T(2,128)(2,1)S(1)}, bf16[2,1280]{1,0:T(2,128)(2,1)}, u32[]{:S(2)}) copy-start(bf16[2,1280]{1,0:T(2,128)(2,1)} %param.27) | copy-start | bytes 15364
  21.0 6.4 %copy-start.3 = (bf16[2,1280]{1,0:T(2,128)(2,1)S(1)}, bf16[2,1280]{1,0:T(2,128)(2,1)}, u32[]{:S(2)}) copy-start(bf16[2,1280]{1,0:T(2,128)(2,1)} %param.29) | copy-start | bytes 15364
  21.0 6.6 %copy-start.4 = (bf16[2,1280]{1,0:T(2,128)(2,1)S(1)}, bf16[2,1280]{1,0:T(2,128)(2,1)}, u32[]{:S(2)}) copy-start(bf16[2,1280]{1,0:T(2,128)(2,1)} %param.31) | copy-start | bytes 15364
  21.0 6.7 %copy-start.9 = (s32[128]{0:T(128)S(1)}, s32[128]{0:T(128)}, u32[]{:S(2)}) copy-start(s32[128]{0:T(128)} %param.21) | copy-start | bytes 1540
  21.0 32.3 %reduce-scatter.9.cloned.1.call-start = ((), (), s32[]{:S(2)}) async-start(), calls=%async_computation.7 | async-start | bytes 409600 | tf_op jit(solution)/shard_map/reduce_scatter | solution.py:50
  24.2 49.2 %reduce-scatter.11.cloned.1.call-start = ((), (), s32[]{:S(2)}) async-start(), calls=%async_computation.8 | async-start | bytes 409600 | tf_op jit(solution)/shard_map/reduce_scatter | solution.py:50
  27.3 75.3 %all-reduce.7.cloned.1.call-start = ((), (), s32[]{:S(2)}) async-start(), calls=%async_computation.9 | async-start | bytes 327680 | tf_op jit(solution)/shard_map/psum | solution.py:72
  73.3 11.9 %copy-start.5 = (bf16[2,640]{1,0:T(2,128)(2,1)S(1)}, bf16[2,640]{1,0:T(2,128)(2,1)}, u32[]{:S(2)}) copy-start(bf16[2,640]{1,0:T(2,128)(2,1)} %param.33) | copy-start | bytes 7684
  73.3 12.0 %copy-start.7 = (bf16[2,640]{1,0:T(2,128)(2,1)S(1)}, bf16[2,640]{1,0:T(2,128)(2,1)}, u32[]{:S(2)}) copy-start(bf16[2,640]{1,0:T(2,128)(2,1)} %param.35) | copy-start | bytes 7684
  73.3 12.0 %copy-start.8 = (bf16[2,640]{1,0:T(2,128)(2,1)S(1)}, bf16[2,640]{1,0:T(2,128)(2,1)}, u32[]{:S(2)}) copy-start(bf16[2,640]{1,0:T(2,128)(2,1)} %param.34) | copy-start | bytes 7684
  85.1 63.6 %all-reduce.9.cloned.1.call-start = ((), (), s32[]{:S(2)}) async-start(), calls=%async_computation.10 | async-start | bytes 2621440 | tf_op jit(solution)/shard_map/psum | solution.py:76
  109.8 5.3 %copy-start.1 = (bf16[2,5120]{1,0:T(2,128)(2,1)S(1)}, bf16[2,5120]{1,0:T(2,128)(2,1)}, u32[]{:S(2)}) copy-start(bf16[2,5120]{1,0:T(2,128)(2,1)} %param.37) | copy-start | bytes 61444
  115.1 55.2 %all-reduce.11.cloned.1.call-start = ((), (), s32[]{:S(2)}) async-start(), calls=%async_computation.11 | async-start | bytes 327680 | tf_op jit(solution)/shard_map/psum | solution.py:79
  148.7 5.2 %copy-start.6 = (bf16[2,640]{1,0:T(2,128)(2,1)S(1)}, bf16[2,640]{1,0:T(2,128)(2,1)}, u32[]{:S(2)}) copy-start(bf16[2,640]{1,0:T(2,128)(2,1)} %param.39) | copy-start | bytes 7684
  153.9 41.3 %reduce-scatter.13.cloned.1.call-start = ((), (), s32[]{:S(2)}) async-start(), calls=%async_computation.12 | async-start | bytes 409600 | tf_op jit(solution)/shard_map/reduce_scatter | solution.py:50
  180.5 32.0 %reduce-scatter.15.cloned.1.call-start = ((), (), s32[]{:S(2)}) async-start(), calls=%async_computation.13 | async-start | bytes 409600 | tf_op jit(solution)/shard_map/reduce_scatter | solution.py:50
  183.8 46.0 %reduce-scatter.17.cloned.1.call-start = ((), (), s32[]{:S(2)}) async-start(), calls=%async_computation.14 | async-start | bytes 409600 | tf_op jit(solution)/shard_map/reduce_scatter | solution.py:50
  187.2 71.8 %all-reduce.13.cloned.1.call-start = ((), (), s32[]{:S(2)}) async-start(), calls=%async_computation.15 | async-start | bytes 327680 | tf_op jit(solution)/shard_map/psum | solution.py:72
  241.4 63.6 %all-reduce.15.cloned.1.call-start = ((), (), s32[]{:S(2)}) async-start(), calls=%async_computation.16 | async-start | bytes 2621440 | tf_op jit(solution)/shard_map/psum | solution.py:76
  271.3 55.2 %all-reduce.17.cloned.1.call-start = ((), (), s32[]{:S(2)}) async-start(), calls=%async_computation.17 | async-start | bytes 327680 | tf_op jit(solution)/shard_map/psum | solution.py:79
Sparse Core Ops, SparseCore 0:
  21.1 14.8 reduce-scatter.6
  38.5 14.7 reduce-scatter.8
  55.8 14.7 reduce-scatter.10
  85.3 17.3 all-reduce.6
  115.2 33.5 all-reduce.8
  154.0 16.1 all-reduce.10
  180.6 14.5 reduce-scatter.12
  197.7 14.7 reduce-scatter.14
  214.9 14.7 reduce-scatter.16
  241.6 17.2 all-reduce.12
  271.4 33.5 all-reduce.14
  310.3 16.2 all-reduce.16
where the time goes:
time: 336 us; the launch traced here: 335 us
  waiting for transfers between devices  179 us (53%)
  matrix products  80.4 us (24%)
  blocking collectives  43.2 us (13%)
  other arithmetic  16.4 us (5%)
  between operations  14.5 us (4%)
    psum x2, waiting for transfers between devices, local_step(): inner_sum = lax.psum(inner_part, 'row')  67.2 us
    reduce_scatter x6, waiting for transfers between devices, head_projection(): summed = lax.psum_scatter(partial, 'row', scatter_dimension=1, tiled=True)  45.6 us
    psum x2, waiting for transfers between devices, local_step(): projected = lax.psum(proj_part, 'col')  34.7 us
    psum x2, waiting for transfers between devices, local_step(): out_sum = lax.psum(out_part, 'col')  31.3 us
    psum x4, blocking collectives, layer_norm(): stats = lax.psum(stats, 'row')  27 us
    dot_general x2, matrix products, attention(): jnp.einsum('bhs,bhsd->bhd', prob_cache, v_layer, preferred_element_type=j...  19.5 us
    dot_general x6, matrix products, head_projection(): jnp.dot(normed, weight, preferred_element_type=jnp.float32)  18.2 us
    dot_general x2, matrix products, attention(): jnp.einsum('bhd,bhsd->bhs', q_heads, k_layer, preferred_element_type=jnp....  16.9 us
  transfers between devices with their start and end apart: 12, of which 11 were waited for; matrix products, arithmetic and copies ran while one was open for 17% of the time, Pallas kernels for 0%

commit v1 on v0

v1 whole, which is shorter than its diff:
```python
import functools

import jax
import jax.numpy as jnp
from jax import lax
from jax.experimental import pallas as pl
from jax.experimental.pallas import tpu as pltpu
from jax.sharding import PartitionSpec as P

EPS_LN = 1e-5
F32 = jnp.float32
BF16 = jnp.bfloat16
STREAMS = 2
RING = 12
CB = 8
CW = 512
MESH = pl.DeviceIdType.MESH


def fused(dims, hid_ref, len_ref, k_hbm, v_hbm, g1_ref, c1_ref, wq_hbm, bq_ref, wk_hbm, bk_ref, wv_hbm, bv_ref,
          wo_hbm, bo_ref, g2_ref, c2_ref, f1_hbm, bf1_ref, f2_hbm, bf2_ref,
          out_ref, kt_ref, vt_ref,
          kbuf, vbuf, wqkv, wo, wf1, wf2,
          state, ynorm, st_send, st_recv,
          qd_send, qd_recv, q_mine, qx_send, qx_recv,
          qblk, vexp, snew, o_rows, att, kfull, vfull,
          ysend, yrecv, acc,
          fd_send, fd_recv, f_mine, fx_send, fx_recv, u_buf,
          kv_sem, w_sem, st_ssem, st_rsem, qd_ssem, qd_rsem, qx_ssem, qx_rsem,
          at_ssem, at_rsem, y_ssem, y_rsem, fd_ssem, fd_rsem, fx_ssem, fx_rsem, u_ssem, u_rsem):
    layers, batch, dm, hw, heads, s_max = dims
    hd = hw // heads
    d_total = dm * 4
    rows = batch // STREAMS
    nchunk = rows // CB
    total_chunks = layers * STREAMS * nchunk
    ff_half = wf1.shape[1] // 2
    nj = ff_half // CW

    r = lax.axis_index("row")
    c = lax.axis_index("col")
    core = lax.rem(r, 2)
    chip = r // 2
    partner = r + 1 - 2 * core
    xpeer = lax.rem(r + 2, 4)
    diag = lax.rem(partner + 2, 4)
    dev_p = {"row": partner}
    dev_x = {"row": xpeer}
    dev_d = {"row": diag}
    dev_y = {"col": 1 - c}

    def rcopy(src, dst, ssem, rsem, dev):
        return pltpu.make_async_remote_copy(src_ref=src, dst_ref=dst, send_sem=ssem, recv_sem=rsem,
                                            device_id=dev, device_id_type=MESH)

    def kv_copies(ci):
        layer = ci // (STREAMS * nchunk)
        first = lax.rem(ci, STREAMS * nchunk) * CB
        slot = lax.rem(ci, RING)
        return (pltpu.make_async_copy(k_hbm.at[layer, pl.ds(first, CB)], kbuf.at[slot], kv_sem.at[0, slot]),
                pltpu.make_async_copy(v_hbm.at[layer, pl.ds(first, CB)], vbuf.at[slot], kv_sem.at[1, slot]))

    def w_copies(name, layer):
        if name == "qkv":
            return [pltpu.make_async_copy(w.at[layer], wqkv.at[i], w_sem.at[i])
                    for i, w in enumerate((wq_hbm, wk_hbm, wv_hbm))]
        src, dst, i = {"o": (wo_hbm, wo, 3), "f1": (f1_hbm, wf1, 4), "f2": (f2_hbm, wf2, 5)}[name]
        return [pltpu.make_async_copy(src.at[layer], dst, w_sem.at[i])]

    def w_start(name, layer):
        if layer < layers:
            for cp in w_copies(name, layer):
                cp.start()

    def w_wait(name, layer):
        for cp in w_copies(name, layer):
            cp.wait()

    w_start("qkv", 0)

    def prime(ci, carry):
        for cp in kv_copies(ci):
            cp.start()
        return carry

    lax.fori_loop(0, RING, prime, 0)

    barrier = pltpu.get_barrier_semaphore()
    for dev in (dev_p, dev_x, dev_d, dev_y):
        pl.semaphore_signal(barrier, inc=1, device_id=dev, device_id_type=MESH)
    pl.semaphore_wait(barrier, 4)

    def rsl(s):
        return pl.ds(s * rows, rows)

    def stat_copies(s, which):
        return [rcopy(st_send.at[which, s], st_recv.at[which, s, i], st_ssem.at[which, s, i], st_rsem.at[which, s, i], dev)
                for i, dev in enumerate((dev_p, dev_x, dev_d))]

    def stats_send(s, which, xv):
        p1 = xv[:, 0:128]
        p2 = p1 * p1
        for i in range(1, dm // 128):
            t = xv[:, i * 128:(i + 1) * 128]
            p1 = p1 + t
            p2 = p2 + t * t
        both = jnp.concatenate([p1, p2], axis=0)
        row = jnp.sum(both.T, axis=0, keepdims=True)
        st_send[which, s] = jnp.broadcast_to(row, (8, 2 * rows))
        for cp in stat_copies(s, which):
            cp.start()

    def norm(s, which, gain, shift):
        for cp in stat_copies(s, which):
            cp.wait()
        row = ((st_send[which, s, 0:1, :] + st_recv[which, s, 0, 0:1, :])
               + (st_recv[which, s, 1, 0:1, :] + st_recv[which, s, 2, 0:1, :]))
        n2 = 2 * rows
        eye = lax.broadcasted_iota(jnp.int32, (n2, n2), 0) == lax.broadcasted_iota(jnp.int32, (n2, n2), 1)
        col = jnp.sum(jnp.where(eye, jnp.broadcast_to(row, (n2, n2)), 0.0), axis=1, keepdims=True)
        mean = col[0:rows] * (1.0 / d_total)
        var = col[rows:] * (1.0 / d_total) - mean * mean
        rstd = lax.rsqrt(var + EPS_LN)
        xv = state[rsl(s), :].astype(F32)
        ynorm[rsl(s), :] = ((xv - mean) * rstd * gain.astype(F32) + shift.astype(F32)).astype(BF16)

    def qd_copy(s, i):
        return rcopy(qd_send.at[s, i], qd_recv.at[s, i], qd_ssem.at[s, i], qd_rsem.at[s, i], dev_p)

    def qx_copy(s):
        return rcopy(qx_send.at[s], qx_recv.at[s], qx_ssem.at[s], qx_rsem.at[s], dev_x)

    def qkv_part(s, layer):
        yv = ynorm[rsl(s), :]
        for i, target in enumerate((1 - chip, chip)):
            off = pl.multiple_of(target * (2 * hw), 128)
            for m in range(3):
                res = jnp.dot(yv, wqkv[m, :, pl.ds(off, 2 * hw)], preferred_element_type=F32)
                low, high = res[:, :hw], res[:, hw:]
                q_mine[s, i, :, m * hw:(m + 1) * hw] = jnp.where(core == 0, low, high)
                qd_send[s, i, :, m * hw:(m + 1) * hw] = jnp.where(core == 0, high, low).astype(BF16)
            qd_copy(s, i).start()

    def qkv_forward(s):
        qd_copy(s, 0).wait()
        qx_send[s] = (q_mine[s, 0] + qd_recv[s, 0].astype(F32)).astype(BF16)
        qx_copy(s).start()

    def own_bias(b_ref, layer):
        b = b_ref[layer:layer + 1, :].astype(F32)
        parts = [b[:, i * hw:(i + 1) * hw] for i in range(4)]
        return jnp.where(r == 0, parts[0], jnp.where(r == 1, parts[1], jnp.where(r == 2, parts[2], parts[3])))

    def expand_mat(dtype):
        hr = heads * rows
        return (lax.broadcasted_iota(jnp.int32, (hr, rows), 0) // heads
                == lax.broadcasted_iota(jnp.int32, (hr, rows), 1)).astype(F32).astype(dtype)

    def head_mask(n):
        row = lax.rem(lax.broadcasted_iota(jnp.int32, (n, hw), 0), heads)
        lane = lax.broadcasted_iota(jnp.int32, (n, hw), 1)
        return (lane >= row * hd) & (lane < row * hd + hd)

    def qkv_finish(s, layer):
        qd_copy(s, 1).wait()
        qx_copy(s).wait()
        tot = (q_mine[s, 1] + qd_recv[s, 1].astype(F32)) + qx_recv[s].astype(F32)
        q = ((tot[:, 0:hw] + own_bias(bq_ref, layer)) * (hd ** -0.5)).astype(BF16)
        k = (tot[:, hw:2 * hw] + own_bias(bk_ref, layer)).astype(BF16)
        v = (tot[:, 2 * hw:3 * hw] + own_bias(bv_ref, layer)).astype(BF16)
        kfull[rsl(s), :hw] = k.astype(F32)
        vfull[rsl(s), :hw] = v.astype(F32)
        ex = expand_mat(BF16)
        hm = head_mask(heads * rows)
        qe = jnp.where(hm, jnp.dot(ex, q, preferred_element_type=F32), 0.0)
        ke = jnp.dot(ex, k, preferred_element_type=F32)
        vexp[...] = jnp.dot(ex, v, preferred_element_type=F32)
        qblk[...] = qe.astype(BF16)
        snew[...] = jnp.broadcast_to(jnp.sum(qe * ke, axis=1, keepdims=True), snew.shape)

    def attention(s, layer):
        base = (layer * STREAMS + s) * nchunk
        r8 = lax.broadcasted_iota(jnp.int32, (8, 1), 0)
        upper = r8 < heads
        nr = CB * heads
        pos = lax.broadcasted_iota(jnp.int32, (nr, s_max), 1)
        hm = head_mask(nr)

        def body(g, carry):
            ci = base + g
            slot = lax.rem(ci, RING)
            for cp in kv_copies(ci):
                cp.wait()
            row0 = pl.multiple_of(g * nr, nr)
            sc = []
            lens = []
            for t in range(nr // 16):
                lhs = qblk[pl.ds(pl.multiple_of(row0 + t * 16, 16), 16), :]
                d = [jnp.dot(lhs, kbuf[slot, t * 4 + i], preferred_element_type=F32) for i in range(4)]
                sc.append(jnp.where(upper, d[0][0:8], d[1][0:8]))
                sc.append(jnp.where(upper, d[2][8:16], d[3][8:16]))
                ln = [len_ref[s * rows + g * CB + t * 4 + i] for i in range(4)]
                lens.append(jnp.where(upper, ln[0], ln[1]))
                lens.append(jnp.where(upper, ln[2], ln[3]))
            scores = jnp.concatenate(sc, axis=0)
            length = jnp.concatenate(lens, axis=0)
            scores = jnp.where(pos < length, scores, -jnp.inf)
            sn = snew[pl.ds(row0, nr), 0:1]
            peak = jnp.maximum(jnp.max(scores, axis=1, keepdims=True), sn)
            e = jnp.exp(scores - peak)
            en = jnp.exp(sn - peak)
            inv = 1.0 / (jnp.sum(e, axis=1, keepdims=True) + en)
            prob = (e * inv).astype(BF16)
            pn = (en * inv).astype(BF16).astype(F32)
            o = []
            for t in range(nr // 16):
                lhs = prob[t * 16:(t + 1) * 16]
                d = [lax.dot_general(lhs, vbuf[slot, t * 4 + i], (((1,), (1,)), ((), ())), preferred_element_type=F32)
                     for i in range(4)]
                o.append(jnp.where(upper, d[0][0:8], d[1][0:8]))
                o.append(jnp.where(upper, d[2][8:16], d[3][8:16]))
            mixed = jnp.concatenate(o, axis=0) + pn * vexp[pl.ds(row0, nr), :]
            o_rows[pl.ds(row0, nr), :] = jnp.where(hm, mixed, 0.0).astype(BF16)

            @pl.when(ci + RING < total_chunks)
            def _():
                for cp in kv_copies(ci + RING):
                    cp.start()
            return carry

        lax.fori_loop(0, nchunk, body, 0)

    def att_copies(s):
        mine = att.at[s, 0]
        return (rcopy(mine, att.at[s, 1], at_ssem.at[s, 0], at_rsem.at[s, 0], dev_p),
                rcopy(mine, att.at[s, 2], at_ssem.at[s, 1], at_rsem.at[s, 1], dev_x),
                rcopy(att.at[s, 2], att.at[s, 3], at_ssem.at[s, 2], at_rsem.at[s, 2], dev_p))

    def att_send(s):
        hr = heads * rows
        sel = (lax.broadcasted_iota(jnp.int32, (rows, hr), 1) // heads
               == lax.broadcasted_iota(jnp.int32, (rows, hr), 0)).astype(F32).astype(BF16)
        att[s, 0] = jnp.dot(sel, o_rows[...], preferred_element_type=F32).astype(BF16)
        a, b, _ = att_copies(s)
        b.start()
        a.start()

    def att_relay(s):
        _, b, f = att_copies(s)
        b.wait_recv()
        f.start()

    def y_copy(s, which):
        return rcopy(ysend.at[which, s], yrecv.at[which, s], y_ssem.at[which, s], y_rsem.at[which, s], dev_y)

    def out_proj(s):
        a, b, f = att_copies(s)
        a.wait()
        b.wait_send()
        f.wait()
        res = None
        for i, owner in enumerate((r, partner, xpeer, diag)):
            off = pl.multiple_of(owner * hw, 16)
            t = jnp.dot(att[s, i], wo[pl.ds(off, hw), :], preferred_element_type=F32)
            res = t if res is None else res + t
        ysend[0, s] = res.astype(BF16)
        y_copy(s, 0).start()

    def residual(s, which, bias):
        y_copy(s, which).wait()
        both = ysend[which, s].astype(F32) + yrecv[which, s].astype(F32)
        new = (state[rsl(s), :].astype(F32) + (both + bias.astype(F32))).astype(BF16)
        return new

    def fd_copy(s, j):
        return rcopy(fd_send.at[s, j], fd_recv.at[s, j], fd_ssem.at[s, j], fd_rsem.at[s, j], dev_p)

    def fx_copy(s, j):
        return rcopy(fx_send.at[s, j], fx_recv.at[s, j], fx_ssem.at[s, j], fx_rsem.at[s, j], dev_x)

    def u_copy(s, j, owner):
        return rcopy(u_buf.at[s, owner, j], u_buf.at[s, owner, j], u_ssem.at[s, j], u_rsem.at[s, j], dev_p)

    def fc1_part(s):
        yv = ynorm[rsl(s), :]

        def body(j, carry):
            off = pl.multiple_of((1 - core) * ff_half + j * CW, 128)
            fd_send[s, j] = jnp.dot(yv, wf1[:, pl.ds(off, CW)], preferred_element_type=F32).astype(BF16)
            fd_copy(s, j).start()
            off = pl.multiple_of(core * ff_half + j * CW, 128)
            f_mine[s, j] = jnp.dot(yv, wf1[:, pl.ds(off, CW)], preferred_element_type=F32)
            return carry

        lax.fori_loop(0, nj, body, 0)

    def fc1_forward(s):
        def body(j, carry):
            fd_copy(s, j).wait()
            fx_send[s, j] = (f_mine[s, j] + fd_recv[s, j].astype(F32)).astype(BF16)
            fx_copy(s, j).start()
            return carry

        lax.fori_loop(0, nj, body, 0)

    def fc2_add(s, j, owner):
        off = pl.multiple_of(owner * ff_half + j * CW, 128)
        acc[s] += jnp.dot(u_buf[s, owner, j], wf2[pl.ds(off, CW), :], preferred_element_type=F32)

    def mlp(s, layer, lo, hi):
        if lo == 0:
            acc[s] = jnp.zeros(acc.shape[1:], F32)

        def body(j, carry):
            fx_copy(s, j).wait()
            off = pl.multiple_of(core * ff_half + j * CW, 128)
            bias = bf1_ref[layer:layer + 1, pl.ds(off, CW)].astype(F32)
            u = ((fx_send[s, j].astype(F32) + fx_recv[s, j].astype(F32)) + bias).astype(BF16)
            u_buf[s, core, j] = jnp.maximum(u, jnp.zeros_like(u))
            u_copy(s, j, core).start()
            fc2_add(s, j, core)

            @pl.when(j > 0)
            def _():
                u_copy(s, j - 1, 1 - core).wait_recv()
                fc2_add(s, j - 1, 1 - core)
            return carry

        lax.fori_loop(lo, hi, body, 0)
        if hi == nj:
            u_copy(s, nj - 1, 1 - core).wait_recv()
            fc2_add(s, nj - 1, 1 - core)

            def drain(j, carry):
                u_copy(s, j, core).wait_send()
                return carry

            lax.fori_loop(0, nj, drain, 0)
            ysend[1, s] = acc[s].astype(BF16)
            y_copy(s, 1).start()

    def kv_out(layer):
        kt_ref[layer] = kfull[...].T[:hw, :].astype(BF16)
        vt_ref[layer] = vfull[...].T[:hw, :].astype(BF16)

    kfull[...] = jnp.zeros_like(kfull)
    vfull[...] = jnp.zeros_like(vfull)
    state[...] = hid_ref[...]
    S = range(STREAMS)
    for s in S:
        stats_send(s, 0, state[rsl(s), :].astype(F32))
    for layer in range(layers):
        last = layer == layers - 1
        w_wait("qkv", layer)
        for s in S:
            norm(s, 0, g1_ref[layer:layer + 1, :], c1_ref[layer:layer + 1, :])
            qkv_part(s, layer)
        w_start("qkv", layer + 1)
        if layer == 0:
            w_start("o", 0)
            w_start("f1", 0)
            w_start("f2", 0)
        for s in S:
            qkv_forward(s)
        for s in S:
            qkv_finish(s, layer)
            attention(s, layer)
            att_send(s)
        kv_out(layer)
        for s in S:
            att_relay(s)
        w_wait("o", layer)
        for s in S:
            out_proj(s)
        w_start("o", layer + 1)
        for s in S:
            new = residual(s, 0, bo_ref[layer:layer + 1, :])
            state[rsl(s), :] = new
            stats_send(s, 1, new.astype(F32))
        w_wait("f1", layer)
        for s in S:
            norm(s, 1, g2_ref[layer:layer + 1, :], c2_ref[layer:layer + 1, :])
            fc1_part(s)
            fc1_forward(s)
        w_start("f1", layer + 1)
        w_wait("f2", layer)
        for s in S:
            mlp(s, layer, 0, nj)
        w_start("f2", layer + 1)
        for s in S:
            new = residual(s, 1, bf2_ref[layer:layer + 1, :])
            if last:
                out_ref[rsl(s), :] = new
            else:
                state[rsl(s), :] = new
                stats_send(s, 0, new.astype(F32))


def solution(mesh):
    act_spec = P("dp", "row")
    cache_spec = P(None, "dp", ("col", "row"), None, None)
    fresh_spec = P(None, "dp", ("col", "row"), None)
    in_weight = P(None, "row", "col")
    out_weight = P(None, "col", "row")
    col_vec = P(None, "col")
    row_vec = P(None, "row")
    in_specs = (act_spec, P("dp"), cache_spec, cache_spec, row_vec, row_vec,
                in_weight, col_vec, in_weight, col_vec, in_weight, col_vec,
                out_weight, row_vec, row_vec, row_vec, in_weight, col_vec, out_weight, row_vec)

    def local_step(hidden, cache_len, k_cache, v_cache, ln1_g, ln1_b, w_q, b_q, w_k, b_k, w_v, b_v,
                   w_o, b_o, ln2_g, ln2_b, w_fc1, b_fc1, w_fc2, b_fc2):
        layers, batch, heads, s_max, hd = k_cache.shape
        dm = hidden.shape[1]
        hw = heads * hd
        ff = w_fc1.shape[2]
        rows = batch // STREAMS
        nj = ff // 2 // CW
        kt = k_cache.transpose(0, 1, 2, 4, 3).reshape(layers, batch, hw, s_max)
        vt = v_cache.transpose(0, 1, 2, 4, 3).reshape(layers, batch, hw, s_max)
        vm = pl.BlockSpec(memory_space=pltpu.VMEM)
        hb = pl.BlockSpec(memory_space=pl.ANY)
        sm = pl.BlockSpec(memory_space=pltpu.SMEM)
        hr = heads * rows
        V = pltpu.VMEM
        D = pltpu.SemaphoreType.DMA
        scratch = [
            V((RING, CB, hw, s_max), BF16), V((RING, CB, hw, s_max), BF16),
            V((3,) + w_q.shape[1:], BF16), V(w_o.shape[1:], BF16), V(w_fc1.shape[1:], BF16), V(w_fc2.shape[1:], BF16),
            V((batch, dm), BF16), V((batch, dm), BF16),
            V((2, STREAMS, 8, 2 * rows), F32), V((2, STREAMS, 3, 8, 2 * rows), F32),
            V((STREAMS, 2, rows, 3 * hw), BF16), V((STREAMS, 2, rows, 3 * hw), BF16), V((STREAMS, 2, rows, 3 * hw), F32),
            V((STREAMS, rows, 3 * hw), BF16), V((STREAMS, rows, 3 * hw), BF16),
            V((hr, hw), BF16), V((hr, hw), F32), V((hr, 128), F32), V((hr, hw), BF16),
            V((STREAMS, 4, rows, hw), BF16), V((batch, 384), F32), V((batch, 384), F32),
            V((2, STREAMS, rows, dm), BF16), V((2, STREAMS, rows, dm), BF16), V((STREAMS, rows, dm), F32),
            V((STREAMS, nj, rows, CW), BF16), V((STREAMS, nj, rows, CW), BF16), V((STREAMS, nj, rows, CW), F32),
            V((STREAMS, nj, rows, CW), BF16), V((STREAMS, nj, rows, CW), BF16), V((STREAMS, 2, nj, rows, CW), BF16),
            D((2, RING)), D((6,)), D((2, STREAMS, 3)), D((2, STREAMS, 3)),
            D((STREAMS, 2)), D((STREAMS, 2)), D((STREAMS,)), D((STREAMS,)),
            D((STREAMS, 3)), D((STREAMS, 3)), D((2, STREAMS)), D((2, STREAMS)),
            D((STREAMS, nj)), D((STREAMS, nj)), D((STREAMS, nj)), D((STREAMS, nj)), D((STREAMS, nj)), D((STREAMS, nj)),
        ]
        out, kn, vn = pl.pallas_call(
            functools.partial(fused, (layers, batch, dm, hw, heads, s_max)),
            out_shape=(jax.ShapeDtypeStruct((batch, dm), BF16),
                       jax.ShapeDtypeStruct((layers, hw, batch), BF16),
                       jax.ShapeDtypeStruct((layers, hw, batch), BF16)),
            in_specs=[vm, sm, hb, hb, vm, vm, hb, vm, hb, vm, hb, vm, hb, vm, vm, vm, hb, vm, hb, vm],
            out_specs=(vm, vm, vm),
            scratch_shapes=scratch,
            compiler_params=pltpu.CompilerParams(collective_id=0, has_side_effects=True,
                                                 vmem_limit_bytes=67043328),
        )(hidden, cache_len, kt, vt, ln1_g, ln1_b, w_q, b_q, w_k, b_k, w_v, b_v,
          w_o, b_o, ln2_g, ln2_b, w_fc1, b_fc1, w_fc2, b_fc2)
        kn = kn.reshape(layers, heads, hd, batch).transpose(0, 3, 1, 2)
        vn = vn.reshape(layers, heads, hd, batch).transpose(0, 3, 1, 2)
        return out, kn, vn

    return jax.shard_map(local_step, mesh=mesh, in_specs=in_specs,
                         out_specs=(act_spec, fresh_spec, fresh_spec), check_vma=False)
```

time: 336 us -> 137 us (0.41)
  waiting for transfers between devices: 179 us -> 0 us
  Pallas kernels: 0 us -> 132 us
  matrix products: 80.4 us -> 0 us
  blocking collectives: 43.2 us -> 0 us
  other arithmetic: 16.4 us -> 0 us
  between operations: 14.5 us -> 0.65 us
  local copies, waits for them, and re-layouts: 0.72 us -> 4.78 us
    psum x6 -> x0, waiting for transfers between devices: 133 us -> none  [the longest x2 67.2 us: local_step(): inner_sum = lax.psum(inner_part, 'row')]
    pallas_call x0 -> x1, Pallas kernels: none -> 132 us  [local_step(): pl.pallas_call(functools.partial(fused, (layers, batch, dm, hw, heads, s_...]
    dot_general x16 -> x0, matrix products: 80.4 us -> none  [the longest x2 19.5 us: attention(): jnp.einsum('bhs,bhsd->bhd', prob_cache, v_layer, preferred_element_type=j...]
    reduce_scatter x6 -> x0, waiting for transfers between devices: 45.6 us -> none  [head_projection(): summed = lax.psum_scatter(partial, 'row', scatter_dimension=1, tiled=True)]
    psum x4 -> x0, blocking collectives: 27 us -> none  [layer_norm(): stats = lax.psum(stats, 'row')]
    all_gather x2 -> x0, blocking collectives: 16.2 us -> none  [local_step(): lax.all_gather(attended.reshape(batch_rows, heads_dev * head_dim), 'row',...]
    convert_element_type x13 -> x0, other arithmetic: 8.1 us -> none  [the longest x6 5.96 us: head_projection(): ((summed.astype(jnp.float32) + bias_own.astype(jnp.float32)) * scale).ast...]
    reduce_sum x6 -> x0, other arithmetic: 4.84 us -> none  [the longest x4 4.29 us: layer_norm(): jnp.sum(state_f32, axis=-1)]
  transfers between devices with their start and end apart: 12 -> 0, of which waited for: 11 -> 0; matrix products, arithmetic and copies ran while one was open for 17% -> 0% of each run, Pallas kernels for 0% -> 0%
where the time goes in v1:
time: 137 us
  Pallas kernels  132 us (96%)
  local copies, waits for them, and re-layouts  4.78 us (3%)
    pallas_call x1, Pallas kernels, local_step(): pl.pallas_call(functools.partial(fused, (layers, batch, dm, hw, heads, s_...  132 us
    unnamed x3, local copies, waits for them, and re-layouts  4.78 us

profile of v1, /device:TPU:0, one launch (start us, length us, event | category | flops | bytes accessed | tf_op | source)
XLA Modules:
  0.0 137.0 jit_solution(14149232638105309633)
XLA Ops:
  0.6 131.5 %shard_map.211 = (bf16[128,640]{1,0:T(8,128)(2,1)}, bf16[2,320,128]{2,1,0:T(8,128)(2,1)}, bf16[2,320,128]{2,1,0:T(8,128)(2,1)}) custom-call(bf16[128,640]{1,0:T(8,128)(2,1)} %hid_ref.1, s32[128]{0:T(128)} %len_ref.1, bf16[2,128,320,256]{3,2,1,0:T(8,128)(2,1)} %bitcast.12, bf16[2,128,320,256]{3,2,1,0:T(8,128)(2,1)} %bitcast.13, bf16[2,640]{1,0:T(2,128)(2,1)} %g1_ref.1, ...), custom_call_target="tpu_custom_call" | custom-call | tf_op jit(solution)/shard_map/pallas_call | solution.py:444
  132.2 1.6 %copy.26 = bf16[128,640]{1,0:T(8,128)(2,1)} copy(bf16[128,640]{1,0:T(8,128)(2,1)} %get-tuple-element.12) | data formatting | bytes 327680
  133.8 1.6 %copy.27 = bf16[2,128,4,80]{1,3,2,0:T(8,128)(2,1)} copy(bf16[2,128,4,80]{1,3,2,0:T(8,128)(2,1)} %bitcast.15) | data formatting | bytes 327680
  135.4 1.6 %copy.28 = bf16[2,128,4,80]{1,3,2,0:T(8,128)(2,1)} copy(bf16[2,128,4,80]{1,3,2,0:T(8,128)(2,1)} %bitcast.14) | data formatting | bytes 327680

commit v2 on v1

v2 whole, which is shorter than its diff:
```python
import functools

import jax
import jax.numpy as jnp
from jax import lax
from jax.experimental import pallas as pl
from jax.experimental.pallas import tpu as pltpu
from jax.sharding import PartitionSpec as P

EPS_LN = 1e-5
F32 = jnp.float32
BF16 = jnp.bfloat16
STREAMS = 2
RING = 12
CB = 8
CW = 512
MESH = pl.DeviceIdType.MESH
LANES = 128


def wide(tiles):
    return jnp.concatenate(tiles, axis=1)


def fused(dims, hid_ref, len_ref, k_hbm, v_hbm, g1_ref, c1_ref, wq_hbm, bq_ref, wk_hbm, bk_ref, wv_hbm, bv_ref,
          wo_hbm, bo_ref, g2_ref, c2_ref, f1_hbm, bf1_ref, f2_hbm, bf2_ref,
          out_ref, kt_ref, vt_ref,
          kbuf, vbuf, wqkv, wo, wf1, wf2,
          state, ynorm, st_send, st_recv,
          qd_send, qd_recv, q_mine, qx_send, qx_recv,
          qblk, snew, sbuf, pbuf, pnew, tmix, att, kfull, vfull,
          ysend, yrecv, acc,
          fd_send, fd_recv, f_mine, fx_send, fx_recv, u_buf,
          kv_sem, wq_sem, wo_sem, f1_sem, f2_sem, st_ssem, st_rsem, qd_ssem, qd_rsem, qx_ssem, qx_rsem,
          at_ssem, at_rsem, y_ssem, y_rsem, fd_ssem, fd_rsem, fx_ssem, fx_rsem, u_ssem, u_rsem):
    layers, batch, dm, hw, heads, s_max, ff = dims
    hd = hw // heads
    d_total = dm * 4
    rows = batch // STREAMS
    nchunk = rows // CB
    total_chunks = layers * STREAMS * nchunk
    ff_half = ff // 2
    nt = dm // LANES
    ct = CW // LANES
    nj = ff_half // CW

    r = lax.axis_index("row")
    c = lax.axis_index("col")
    core = lax.rem(r, 2)
    chip = r // 2
    partner = r + 1 - 2 * core
    xpeer = lax.rem(r + 2, 4)
    diag = lax.rem(partner + 2, 4)
    dev_p = {"row": partner}
    dev_x = {"row": xpeer}
    dev_d = {"row": diag}
    dev_y = {"col": 1 - c}

    def rcopy(src, dst, ssem, rsem, dev):
        return pltpu.make_async_remote_copy(src_ref=src, dst_ref=dst, send_sem=ssem, recv_sem=rsem,
                                            device_id=dev, device_id_type=MESH)

    def kv_copies(ci, i):
        layer = ci // (STREAMS * nchunk)
        first = lax.rem(ci, STREAMS * nchunk) * CB
        slot = lax.rem(ci, RING)
        src, dst = ((k_hbm, kbuf), (v_hbm, vbuf))[i]
        return [pltpu.make_async_copy(src.at[layer, pl.ds(first, CB), :, pl.ds(h * LANES, LANES)], dst.at[slot, :, h],
                                      kv_sem.at[i, h, slot]) for h in range(s_max // LANES)]

    def kv_start(ci, i):
        for cp in kv_copies(ci, i):
            cp.start()

    def kv_wait(ci, i):
        for cp in kv_copies(ci, i):
            cp.wait()

    def w_each(name, layer, act):
        def run(src, dst, sems, tiles):
            def body(t, carry):
                cp = pltpu.make_async_copy(src.at[layer, :, pl.ds(pl.multiple_of(t * LANES, LANES), LANES)], dst(t), sems(t))
                cp.start() if act else cp.wait()
                return carry
            lax.fori_loop(0, tiles, body, 0)

        if name == "qkv":
            for i, w in enumerate((wq_hbm, wk_hbm, wv_hbm)):
                run(w, lambda t, i=i: wqkv.at[t // nt, i * nt + lax.rem(t, nt)], lambda t, i=i: wq_sem.at[i, t], 2 * nt)
        elif name == "o":
            run(wo_hbm, lambda t: wo.at[t], lambda t: wo_sem.at[t], nt)
        elif name == "f1":
            run(f1_hbm, lambda t: wf1.at[t], lambda t: f1_sem.at[t], ff // LANES)
        else:
            run(f2_hbm, lambda t: wf2.at[t], lambda t: f2_sem.at[t], nt)

    def w_start(name, layer):
        if layer < layers:
            w_each(name, layer, True)

    def w_wait(name, layer):
        w_each(name, layer, False)

    w_start("qkv", 0)

    def prime(ci, carry):
        kv_start(ci, 0)
        kv_start(ci, 1)
        return carry

    lax.fori_loop(0, RING, prime, 0)

    barrier = pltpu.get_barrier_semaphore()
    for dev in (dev_p, dev_x, dev_d, dev_y):
        pl.semaphore_signal(barrier, inc=1, device_id=dev, device_id_type=MESH)
    pl.semaphore_wait(barrier, 4)

    def rsl(s):
        return pl.ds(s * rows, rows)

    def stat_copies(s, which):
        return [rcopy(st_send.at[which, s], st_recv.at[which, s, i], st_ssem.at[which, s, i], st_rsem.at[which, s, i], dev)
                for i, dev in enumerate((dev_p, dev_x, dev_d))]

    def stats_send(s, which, xv):
        p1 = xv[:, 0:128]
        p2 = p1 * p1
        for i in range(1, dm // 128):
            t = xv[:, i * 128:(i + 1) * 128]
            p1 = p1 + t
            p2 = p2 + t * t
        both = jnp.concatenate([p1, p2], axis=0)
        row = jnp.sum(both.T, axis=0, keepdims=True)
        st_send[which, s] = jnp.broadcast_to(row, (8, 2 * rows))
        for cp in stat_copies(s, which):
            cp.start()

    def norm(s, which, gain, shift):
        for cp in stat_copies(s, which):
            cp.wait()
        row = ((st_send[which, s, 0:1, :] + st_recv[which, s, 0, 0:1, :])
               + (st_recv[which, s, 1, 0:1, :] + st_recv[which, s, 2, 0:1, :]))
        n2 = 2 * rows
        eye = lax.broadcasted_iota(jnp.int32, (n2, n2), 0) == lax.broadcasted_iota(jnp.int32, (n2, n2), 1)
        col = jnp.sum(jnp.where(eye, jnp.broadcast_to(row, (n2, n2)), 0.0), axis=1, keepdims=True)
        mean = col[0:rows] * (1.0 / d_total)
        var = col[rows:] * (1.0 / d_total) - mean * mean
        rstd = lax.rsqrt(var + EPS_LN)
        xv = state[rsl(s), :].astype(F32)
        y = ((xv - mean) * rstd * gain.astype(F32) + shift.astype(F32)).astype(BF16)
        for t in range(nt):
            ynorm[t, rsl(s), :] = y[:, t * LANES:(t + 1) * LANES]

    def normed(s):
        return wide([ynorm[t, rsl(s), :] for t in range(nt)])

    def qd_copy(s, i):
        return rcopy(qd_send.at[s, i], qd_recv.at[s, i], qd_ssem.at[s, i], qd_rsem.at[s, i], dev_p)

    def qx_copy(s):
        return rcopy(qx_send.at[s], qx_recv.at[s], qx_ssem.at[s], qx_rsem.at[s], dev_x)

    def qkv_part(s, i):
        target = 1 - chip if i == 0 else chip
        res = jnp.dot(normed(s), wide([wqkv[target, t] for t in range(3 * nt)]), preferred_element_type=F32)
        for m in range(3):
            low, high = res[:, 2 * m * hw:(2 * m + 1) * hw], res[:, (2 * m + 1) * hw:(2 * m + 2) * hw]
            q_mine[s, i, :, m * hw:(m + 1) * hw] = jnp.where(core == 0, low, high)
            qd_send[s, i, :, m * hw:(m + 1) * hw] = jnp.where(core == 0, high, low).astype(BF16)
        qd_copy(s, i).start()

    def qkv_forward(s):
        qd_copy(s, 0).wait()
        qx_send[s] = (q_mine[s, 0] + qd_recv[s, 0].astype(F32)).astype(BF16)
        qx_copy(s).start()

    def own_bias(b_ref, layer):
        b = b_ref[layer:layer + 1, :].astype(F32)
        parts = [b[:, i * hw:(i + 1) * hw] for i in range(4)]
        return jnp.where(r == 0, parts[0], jnp.where(r == 1, parts[1], jnp.where(r == 2, parts[2], parts[3])))

    def expand_mat():
        hr = heads * rows
        return (lax.broadcasted_iota(jnp.int32, (hr, rows), 0) // heads
                == lax.broadcasted_iota(jnp.int32, (hr, rows), 1)).astype(F32).astype(BF16)

    def head_mask(n):
        row = lax.rem(lax.broadcasted_iota(jnp.int32, (n, hw), 0), heads)
        lane = lax.broadcasted_iota(jnp.int32, (n, hw), 1)
        return (lane >= row * hd) & (lane < row * hd + hd)

    def qkv_finish(s, layer):
        qd_copy(s, 1).wait()
        qx_copy(s).wait()
        tot = (q_mine[s, 1] + qd_recv[s, 1].astype(F32)) + qx_recv[s].astype(F32)
        q = ((tot[:, 0:hw] + own_bias(bq_ref, layer)) * (hd ** -0.5)).astype(BF16)
        k = (tot[:, hw:2 * hw] + own_bias(bk_ref, layer)).astype(BF16)
        v = (tot[:, 2 * hw:3 * hw] + own_bias(bv_ref, layer)).astype(BF16)
        kfull[rsl(s), :hw] = k.astype(F32)
        vfull[rsl(s), :hw] = v.astype(F32)
        ex = expand_mat()
        hm = head_mask(heads * rows)
        qe = jnp.where(hm, jnp.dot(ex, q, preferred_element_type=F32), 0.0)
        ke = jnp.dot(ex, k, preferred_element_type=F32)
        qblk[...] = qe.astype(BF16)
        snew[...] = jnp.broadcast_to(jnp.sum(qe * ke, axis=1, keepdims=True), snew.shape)

    nr = CB * heads
    per = 128 // nr
    upper = lax.broadcasted_iota(jnp.int32, (8, 1), 0) < heads

    pos = lax.broadcasted_iota(jnp.int32, (nr, s_max), 1)

    def at_row(g):
        return pl.multiple_of(g * nr, nr)

    def scores_of(base, g):
        slot = lax.rem(base + g, RING)
        out = []
        for t in range(nr // 16):
            lhs = qblk[pl.ds(pl.multiple_of(at_row(g) + t * 16, 16), 16), :]
            d = [jnp.dot(lhs, wide([kbuf[slot, t * 4 + i, h] for h in range(s_max // LANES)]), preferred_element_type=F32)
                 for i in range(4)]
            out.append(jnp.where(upper, d[0][0:8], d[1][0:8]))
            out.append(jnp.where(upper, d[2][8:16], d[3][8:16]))
        return jnp.concatenate(out, axis=0)

    def softmax_of(s, g, sc):
        lens = []
        for i in range(0, CB, 2):
            b = s * rows + g * CB + i
            lens.append(jnp.where(upper, len_ref[b], len_ref[b + 1]))
        sc = jnp.where(pos < jnp.concatenate(lens, axis=0), sc, -jnp.inf)
        sn = snew[pl.ds(at_row(g), nr), 0:1]
        peak = jnp.maximum(jnp.max(sc, axis=1, keepdims=True), sn)
        e = jnp.exp(sc - peak)
        en = jnp.exp(sn - peak)
        inv = 1.0 / (jnp.sum(e, axis=1, keepdims=True) + en)
        return (e * inv).astype(BF16), jnp.broadcast_to(en * inv, (nr, LANES))

    def keep_probs(g, prob, fresh):
        for h in range(s_max // LANES):
            pbuf[h, pl.ds(at_row(g), nr), :] = prob[:, h * LANES:(h + 1) * LANES]
        pnew[pl.ds(at_row(g), nr), :] = fresh

    def probs_of(g):
        return wide([pbuf[h, pl.ds(pl.multiple_of(g // per * 128, 128), 128), :] for h in range(s_max // LANES)])

    def mix(base, g, rhs, new):
        slot = lax.rem(base + g, RING)
        seq = lax.broadcasted_iota(jnp.int32, (hw, 128), 1) // heads - lax.rem(g, per) * CB
        for b in range(CB):
            o = lax.dot_general(wide([vbuf[slot, b, h] for h in range(s_max // LANES)]), rhs, (((1,), (1,)), ((), ())),
                                preferred_element_type=F32)
            new = jnp.where(seq == b, o, new)
        return new

    def refill(ci, i):
        @pl.when(ci + RING < total_chunks)
        def _():
            kv_start(ci + RING, i)

    def attention_pair(s, layer, g, tail):
        base = (layer * STREAMS + s) * nchunk
        kv_wait(base + g, 1)
        kv_wait(base + g + 1, 1)
        if not tail:
            kv_wait(base + g + 2, 0)
            kv_wait(base + g + 3, 0)
        sc = sbuf[...]
        rhs = probs_of(g)
        new = tmix[g // per]
        pa = softmax_of(s, g + 1, sc)
        if not tail:
            sc = scores_of(base, g + 2)
        new = mix(base, g, rhs, new)
        keep_probs(g + 1, *pa)
        rhs = probs_of(g + 1)
        if not tail:
            pa = softmax_of(s, g + 2, sc)
            sc = scores_of(base, g + 3)
        new = mix(base, g + 1, rhs, new)
        tmix[g // per] = new
        if not tail:
            keep_probs(g + 2, *pa)
            sbuf[...] = sc
        for k in range(2):
            refill(base + g + k, 1)
            if not tail:
                refill(base + g + 2 + k, 0)

    def attention(s, layer, lo, hi):
        base = (layer * STREAMS + s) * nchunk
        if lo == 0:
            kv_wait(base, 0)
            kv_wait(base + 1, 0)
            pa = softmax_of(s, 0, scores_of(base, 0))
            sbuf[...] = scores_of(base, 1)
            keep_probs(0, *pa)
            refill(base, 0)
            refill(base + 1, 0)

        def body(p, carry):
            attention_pair(s, layer, 2 * p, False)
            return carry

        stop = min(hi, nchunk - 2) // 2
        if stop - lo // 2 > 1:
            lax.fori_loop(lo // 2, stop, body, 0)
        elif stop > lo // 2:
            attention_pair(s, layer, lo, False)
        if hi == nchunk:
            attention_pair(s, layer, nchunk - 2, True)

    def att_copy(s, i):
        src, dev = ((0, dev_p), (0, dev_x), (2, dev_p))[i]
        return rcopy(att.at[s, src], att.at[s, i + 1], at_ssem.at[s, i], at_rsem.at[s, i], dev)

    def att_send(s):
        hr = heads * rows
        sel = (lax.broadcasted_iota(jnp.int32, (rows, hr), 1) // heads
               == lax.broadcasted_iota(jnp.int32, (rows, hr), 0)).astype(F32).astype(BF16)
        pe = jnp.where(head_mask(hr), jnp.broadcast_to(pnew[:, 0:1], (hr, hw)), 0.0).astype(BF16)
        o = jnp.dot(sel, pe, preferred_element_type=F32) * vfull[rsl(s), :hw]
        feat = lax.broadcasted_iota(jnp.int32, (hw, 128), 0)
        lane = lax.rem(lax.broadcasted_iota(jnp.int32, (hw, 128), 1), heads)
        own = (feat >= lane * hd) & (feat < lane * hd + hd)
        for half in range(hr // 128):
            t = jnp.where(own, tmix[half], 0.0)
            high = t.astype(BF16)
            low = (t - high.astype(F32)).astype(BF16)
            pick = sel[:, half * 128:(half + 1) * 128]
            for part in (high, low):
                o = o + lax.dot_general(pick, part, (((1,), (1,)), ((), ())), preferred_element_type=F32)
        att[s, 0] = o.astype(BF16)
        att_copy(s, 1).start()
        att_copy(s, 0).start()

    def att_relay(s):
        att_copy(s, 1).wait_recv()
        att_copy(s, 2).start()

    def y_copy(s, which):
        return rcopy(ysend.at[which, s], yrecv.at[which, s], y_ssem.at[which, s], y_rsem.at[which, s], dev_y)

    def out_proj(s):
        att_copy(s, 0).wait()
        att_copy(s, 1).wait_send()
        att_copy(s, 2).wait()
        res = None
        for i, owner in enumerate((r, partner, xpeer, diag)):
            off = pl.multiple_of(owner * hw, 16)
            t = jnp.dot(att[s, i], wide([wo[n, pl.ds(off, hw), :] for n in range(nt)]), preferred_element_type=F32)
            res = t if res is None else res + t
        ysend[0, s] = res.astype(BF16)
        y_copy(s, 0).start()

    def residual(s, which, bias):
        y_copy(s, which).wait()
        both = ysend[which, s].astype(F32) + yrecv[which, s].astype(F32)
        new = (state[rsl(s), :].astype(F32) + (both + bias.astype(F32))).astype(BF16)
        return new

    def fd_copy(s, j):
        return rcopy(fd_send.at[s, j], fd_recv.at[s, j], fd_ssem.at[s, j], fd_rsem.at[s, j], dev_p)

    def fx_copy(s, j):
        return rcopy(fx_send.at[s, j], fx_recv.at[s, j], fx_ssem.at[s, j], fx_rsem.at[s, j], dev_x)

    def u_copy(s, j, owner):
        return rcopy(u_buf.at[s, owner, j], u_buf.at[s, owner, j], u_ssem.at[s, j], u_rsem.at[s, j], dev_p)

    def fc1_part(s):
        yv = normed(s)

        def columns(owner, j):
            first = owner * (ff_half // LANES) + j * ct
            return jnp.dot(yv, wide([wf1[first + t] for t in range(ct)]), preferred_element_type=F32)

        for j in range(nj):
            res = columns(1 - core, j).astype(BF16)
            for t in range(ct):
                fd_send[s, j, t] = res[:, t * LANES:(t + 1) * LANES]
            fd_copy(s, j).start()
            f_mine[s, j] = columns(core, j)

    def fc1_forward(s, lo, hi):
        def body(j, carry):
            fd_copy(s, j).wait()
            for t in range(ct):
                fx_send[s, j, t] = (f_mine[s, j, :, t * LANES:(t + 1) * LANES] + fd_recv[s, j, t].astype(F32)).astype(BF16)
            fx_copy(s, j).start()
            return carry

        lax.fori_loop(lo, hi, body, 0)

    def fc2_add(s, j, owner):
        off = pl.multiple_of(owner * ff_half + j * CW, 128)
        u = wide([u_buf[s, owner, j, t] for t in range(ct)])
        acc[s] += jnp.dot(u, wide([wf2[n, pl.ds(off, CW), :] for n in range(nt)]), preferred_element_type=F32)

    def mlp(s, layer, lo, hi):
        if lo == 0:
            acc[s] = jnp.zeros(acc.shape[1:], F32)

        def body(j, carry):
            fx_copy(s, j).wait()
            off = pl.multiple_of(core * ff_half + j * CW, 128)
            bias = bf1_ref[layer:layer + 1, pl.ds(off, CW)].astype(F32)
            for t in range(ct):
                u = (fx_send[s, j, t].astype(F32) + fx_recv[s, j, t].astype(F32)) + bias[:, t * LANES:(t + 1) * LANES]
                u = u.astype(BF16)
                u_buf[s, core, j, t] = jnp.maximum(u, jnp.zeros_like(u))
            u_copy(s, j, core).start()
            fc2_add(s, j, core)

            @pl.when(j > 0)
            def _():
                u_copy(s, j - 1, 1 - core).wait_recv()
                fc2_add(s, j - 1, 1 - core)
            return carry

        lax.fori_loop(lo, hi, body, 0)
        if hi == nj:
            u_copy(s, nj - 1, 1 - core).wait_recv()
            fc2_add(s, nj - 1, 1 - core)

            def drain(j, carry):
                u_copy(s, j, core).wait_send()
                return carry

            lax.fori_loop(0, nj, drain, 0)
            ysend[1, s] = acc[s].astype(BF16)
            y_copy(s, 1).start()

    def kv_out(layer):
        kt_ref[layer] = kfull[...].T[:hw, :].astype(BF16)
        vt_ref[layer] = vfull[...].T[:hw, :].astype(BF16)

    def gain_ph(s, which, layer):
        g, b = (g1_ref, c1_ref) if which == 0 else (g2_ref, c2_ref)
        norm(s, which, g[layer:layer + 1, :], b[layer:layer + 1, :])

    def mid_ph(s, layer):
        new = residual(s, 0, bo_ref[layer:layer + 1, :])
        state[rsl(s), :] = new
        stats_send(s, 1, new.astype(F32))

    def end_ph(s, layer):
        new = residual(s, 1, bf2_ref[layer:layer + 1, :])
        if layer == layers - 1:
            out_ref[rsl(s), :] = new
        else:
            state[rsl(s), :] = new
            stats_send(s, 0, new.astype(F32))

    kfull[...] = jnp.zeros_like(kfull)
    vfull[...] = jnp.zeros_like(vfull)
    pbuf[...] = jnp.zeros_like(pbuf)
    tmix[...] = jnp.zeros_like(tmix)
    state[...] = hid_ref[...]
    stats_send(0, 0, state[rsl(0), :].astype(F32))
    stats_send(1, 0, state[rsl(1), :].astype(F32))
    w_wait("qkv", 0)
    gain_ph(0, 0, 0)
    qkv_part(0, 0)
    gain_ph(1, 0, 0)
    qkv_part(1, 0)
    qkv_forward(0)
    qkv_part(0, 1)
    qkv_forward(1)
    qkv_part(1, 1)
    w_start("qkv", 1)
    w_start("o", 0)
    w_start("f1", 0)
    w_start("f2", 0)
    qkv_finish(0, 0)
    attention(0, 0, 0, nchunk)
    att_send(0)
    q4 = nchunk // 4
    for layer in range(layers):
        last = layer == layers - 1
        qkv_finish(1, layer)
        attention(1, layer, 0, q4)
        att_relay(0)
        attention(1, layer, q4, 2 * q4)
        w_wait("o", layer)
        out_proj(0)
        attention(1, layer, 2 * q4, 3 * q4)
        kv_out(layer)
        mid_ph(0, layer)
        attention(1, layer, 3 * q4, nchunk)
        att_send(1)
        gain_ph(0, 1, layer)
        w_wait("f1", layer)
        fc1_part(0)
        fc1_forward(0, 0, nj)
        att_relay(1)
        w_wait("f2", layer)
        mlp(0, layer, 0, 1)
        out_proj(1)
        w_start("o", layer + 1)
        mlp(0, layer, 1, 3)
        mid_ph(1, layer)
        mlp(0, layer, 3, nj)
        gain_ph(1, 1, layer)
        fc1_part(1)
        w_start("f1", layer + 1)
        fc1_forward(1, 0, 2)
        end_ph(0, layer)
        fc1_forward(1, 2, nj)
        if not last:
            w_wait("qkv", layer + 1)
            gain_ph(0, 0, layer + 1)
            qkv_part(0, 0)
            qkv_forward(0)
            qkv_part(0, 1)
        mlp(1, layer, 0, nj)
        w_start("f2", layer + 1)
        if not last:
            qkv_finish(0, layer + 1)
            attention(0, layer + 1, 0, q4)
            end_ph(1, layer)
            attention(0, layer + 1, q4, 2 * q4)
            gain_ph(1, 0, layer + 1)
            qkv_part(1, 0)
            qkv_part(1, 1)
            w_start("qkv", layer + 2)
            qkv_forward(1)
            attention(0, layer + 1, 2 * q4, nchunk)
            att_send(0)
        else:
            end_ph(1, layer)


def finish(a_ref, b_ref, c_ref, x_ref, y_ref, z_ref):
    x_ref[...] = a_ref[...]
    y_ref[...] = b_ref[...]
    z_ref[...] = c_ref[...]


def solution(mesh):
    act_spec = P("dp", "row")
    cache_spec = P(None, "dp", ("col", "row"), None, None)
    fresh_spec = P(None, "dp", ("col", "row"), None)
    in_weight = P(None, "row", "col")
    out_weight = P(None, "col", "row")
    col_vec = P(None, "col")
    row_vec = P(None, "row")
    in_specs = (act_spec, P("dp"), cache_spec, cache_spec, row_vec, row_vec,
                in_weight, col_vec, in_weight, col_vec, in_weight, col_vec,
                out_weight, row_vec, row_vec, row_vec, in_weight, col_vec, out_weight, row_vec)

    def local_step(hidden, cache_len, k_cache, v_cache, ln1_g, ln1_b, w_q, b_q, w_k, b_k, w_v, b_v,
                   w_o, b_o, ln2_g, ln2_b, w_fc1, b_fc1, w_fc2, b_fc2):
        layers, batch, heads, s_max, hd = k_cache.shape
        dm = hidden.shape[1]
        hw = heads * hd
        ff = w_fc1.shape[2]
        rows = batch // STREAMS
        nj = ff // 2 // CW
        nt = dm // LANES
        ct = CW // LANES
        kt = k_cache.transpose(0, 1, 2, 4, 3).reshape(layers, batch, hw, s_max)
        vt = v_cache.transpose(0, 1, 2, 4, 3).reshape(layers, batch, hw, s_max)
        vm = pl.BlockSpec(memory_space=pltpu.VMEM)
        hb = pl.BlockSpec(memory_space=pl.ANY)
        sm = pl.BlockSpec(memory_space=pltpu.SMEM)
        hr = heads * rows
        V = pltpu.VMEM
        D = pltpu.SemaphoreType.DMA
        scratch = [
            V((RING, CB, s_max // LANES, hw, LANES), BF16), V((RING, CB, s_max // LANES, hw, LANES), BF16),
            V((2, 3 * nt, dm, LANES), BF16), V((nt, w_o.shape[1], LANES), BF16),
            V((ff // LANES, dm, LANES), BF16), V((nt, ff, LANES), BF16),
            V((batch, dm), BF16), V((nt, batch, LANES), BF16),
            V((2, STREAMS, 8, 2 * rows), F32), V((2, STREAMS, 3, 8, 2 * rows), F32),
            V((STREAMS, 2, rows, 3 * hw), BF16), V((STREAMS, 2, rows, 3 * hw), BF16), V((STREAMS, 2, rows, 3 * hw), F32),
            V((STREAMS, rows, 3 * hw), BF16), V((STREAMS, rows, 3 * hw), BF16),
            V((hr, hw), BF16), V((hr, 128), F32), V((CB * heads, s_max), F32), V((s_max // LANES, hr, LANES), BF16), V((hr, 128), F32),
            V((hr // 128, hw, 128), F32),
            V((STREAMS, 4, rows, hw), BF16), V((batch, 384), F32), V((batch, 384), F32),
            V((2, STREAMS, rows, dm), BF16), V((2, STREAMS, rows, dm), BF16), V((STREAMS, rows, dm), F32),
            V((STREAMS, nj, ct, rows, LANES), BF16), V((STREAMS, nj, ct, rows, LANES), BF16), V((STREAMS, nj, rows, CW), F32),
            V((STREAMS, nj, ct, rows, LANES), BF16), V((STREAMS, nj, ct, rows, LANES), BF16),
            V((STREAMS, 2, nj, ct, rows, LANES), BF16),
            D((2, s_max // LANES, RING)), D((3, 2 * nt)), D((nt,)), D((ff // LANES,)), D((nt,)), D((2, STREAMS, 3)), D((2, STREAMS, 3)),
            D((STREAMS, 2)), D((STREAMS, 2)), D((STREAMS,)), D((STREAMS,)),
            D((STREAMS, 3)), D((STREAMS, 3)), D((2, STREAMS)), D((2, STREAMS)),
            D((STREAMS, nj)), D((STREAMS, nj)), D((STREAMS, nj)), D((STREAMS, nj)), D((STREAMS, nj)), D((STREAMS, nj)),
        ]
        out, kn, vn = pl.pallas_call(
            functools.partial(fused, (layers, batch, dm, hw, heads, s_max, ff)),
            out_shape=(jax.ShapeDtypeStruct((batch, dm), BF16),
                       jax.ShapeDtypeStruct((layers, hw, batch), BF16),
                       jax.ShapeDtypeStruct((layers, hw, batch), BF16)),
            in_specs=[vm, sm, hb, hb, vm, vm, hb, vm, hb, vm, hb, vm, hb, vm, vm, vm, hb, vm, hb, vm],
            out_specs=(vm, vm, vm),
            scratch_shapes=scratch,
            compiler_params=pltpu.CompilerParams(collective_id=0, has_side_effects=True,
                                                 vmem_limit_bytes=67043328),
        )(hidden, cache_len, kt, vt, ln1_g, ln1_b, w_q, b_q, w_k, b_k, w_v, b_v,
          w_o, b_o, ln2_g, ln2_b, w_fc1, b_fc1, w_fc2, b_fc2)
        out, kn, vn = pl.pallas_call(
            finish, out_shape=tuple(jax.ShapeDtypeStruct(a.shape, a.dtype) for a in (out, kn, vn)),
            in_specs=[vm] * 3, out_specs=(vm,) * 3)(out, kn, vn)
        kn = kn.reshape(layers, heads, hd, batch).transpose(0, 3, 1, 2)
        vn = vn.reshape(layers, heads, hd, batch).transpose(0, 3, 1, 2)
        return out, kn, vn

    return jax.shard_map(local_step, mesh=mesh, in_specs=in_specs,
                         out_specs=(act_spec, fresh_spec, fresh_spec), check_vma=False)
```

time: 137 us -> 120 us (0.88)
  Pallas kernels: 132 us -> 120 us
  local copies, waits for them, and re-layouts: 4.78 us -> 0 us
    pallas_call x1, Pallas kernels: 132 us -> 118 us  [local_step(): pl.pallas_call(functools.partial(fused, (layers, batch, dm, hw, heads, s_...]
    unnamed x3 -> x0, local copies, waits for them, and re-layouts: 4.78 us -> none
    pallas_call x0 -> x1, Pallas kernels: none -> 1.86 us  [local_step(): pl.pallas_call(finish, out_shape=tuple((jax.ShapeDtypeStruct(a.shape, a.d...]
where the time goes in v2:
time: 120 us
  Pallas kernels  120 us (100%)
    pallas_call x1, Pallas kernels, local_step(): pl.pallas_call(functools.partial(fused, (layers, batch, dm, hw, heads, s_...  118 us

profile of v2, /device:TPU:0, one launch (start us, length us, event | category | flops | bytes accessed | tf_op | source)
XLA Modules:
  0.0 120.3 jit_solution(16119502852091986239)
XLA Ops:
  0.6 117.8 %shard_map.211 = (bf16[128,640]{1,0:T(8,128)(2,1)}, bf16[2,320,128]{2,1,0:T(8,128)(2,1)}, bf16[2,320,128]{2,1,0:T(8,128)(2,1)}) custom-call(bf16[128,640]{1,0:T(8,128)(2,1)} %hid_ref.1, s32[128]{0:T(128)} %len_ref.1, bf16[2,128,320,256]{3,2,1,0:T(8,128)(2,1)} %bitcast.12, bf16[2,128,320,256]{3,2,1,0:T(8,128)(2,1)} %bitcast.13, bf16[2,640]{1,0:T(2,128)(2,1)} %g1_ref.1, ...), custom_call_target="tpu_custom_call" | custom-call | tf_op jit(solution)/shard_map/pallas_call | solution.py:592
  118.4 1.9 %shard_map.212 = (bf16[128,640]{1,0:T(8,128)(2,1)}, bf16[2,320,128]{2,1,0:T(8,128)(2,1)}, bf16[2,320,128]{2,1,0:T(8,128)(2,1)}) custom-call(bf16[128,640]{1,0:T(8,128)(2,1)} %get-tuple-element.9.a_ref, bf16[2,320,128]{2,1,0:T(8,128)(2,1)} %get-tuple-element.10.b_ref, bf16[2,320,128]{2,1,0:T(8,128)(2,1)} %get-tuple-element.11.c_ref), custom_call_target="tpu_custom_call" | custom-call | tf_op jit(solution)/shard_map/pallas_call | solution.py:604

commit v3 on v2

--- a/solution.py
+++ b/solution.py
@@ -22,16 +22,17 @@
     return jnp.concatenate(tiles, axis=1)
 
 
-def fused(dims, hid_ref, len_ref, k_hbm, v_hbm, g1_ref, c1_ref, wq_hbm, bq_ref, wk_hbm, bk_ref, wv_hbm, bv_ref,
-          wo_hbm, bo_ref, g2_ref, c2_ref, f1_hbm, bf1_ref, f2_hbm, bf2_ref,
+def fused(dims, hid_hbm, len_hbm, k_hbm, v_hbm, g1_hbm, c1_hbm, wq_hbm, bq_hbm, wk_hbm, bk_hbm, wv_hbm, bv_hbm,
+          wo_hbm, bo_hbm, g2_hbm, c2_hbm, f1_hbm, bf1_hbm, f2_hbm, bf2_hbm,
           out_ref, kt_ref, vt_ref,
           kbuf, vbuf, wqkv, wo, wf1, wf2,
+          len_ref, g1_ref, c1_ref, bq_ref, bk_ref, bv_ref, bo_ref, g2_ref, c2_ref, bf1_ref, bf2_ref,
           state, ynorm, st_send, st_recv,
-          qd_send, qd_recv, q_mine, qx_send, qx_recv,
+          qd_send, qd_recv, kd_send, kd_recv, q_mine, qx_send, qx_recv, kx_send, kx_recv,
           qblk, snew, sbuf, pbuf, pnew, tmix, att, kfull, vfull,
           ysend, yrecv, acc,
           fd_send, fd_recv, f_mine, fx_send, fx_recv, u_buf,
-          kv_sem, wq_sem, wo_sem, f1_sem, f2_sem, st_ssem, st_rsem, qd_ssem, qd_rsem, qx_ssem, qx_rsem,
+          in_sem, kv_sem, wq_sem, wo_sem, f1_sem, f2_sem, st_ssem, st_rsem, qd_ssem, qd_rsem, qx_ssem, qx_rsem,
           at_ssem, at_rsem, y_ssem, y_rsem, fd_ssem, fd_rsem, fx_ssem, fx_rsem, u_ssem, u_rsem):
     layers, batch, dm, hw, heads, s_max, ff = dims
     hd = hw // heads
@@ -101,19 +102,21 @@
     def w_wait(name, layer):
         w_each(name, layer, False)
 
+    small = [pltpu.make_async_copy(a, b, in_sem.at[n]) for n, (a, b) in enumerate((
+        (hid_hbm, state), (len_hbm, len_ref), (g1_hbm, g1_ref), (c1_hbm, c1_ref), (bq_hbm, bq_ref), (bk_hbm, bk_ref),
+        (bv_hbm, bv_ref), (bo_hbm, bo_ref), (g2_hbm, g2_ref), (c2_hbm, c2_ref), (bf1_hbm, bf1_ref), (bf2_hbm, bf2_ref)))]
+    small[0].start()
+    barrier = pltpu.get_barrier_semaphore()
+    for dev in (dev_p, dev_x, dev_d, dev_y):
+        pl.semaphore_signal(barrier, inc=1, device_id=dev, device_id_type=MESH)
+    for cp in small[1:]:
+        cp.start()
     w_start("qkv", 0)
 
     def prime(ci, carry):
         kv_start(ci, 0)
         kv_start(ci, 1)
         return carry
-
-    lax.fori_loop(0, RING, prime, 0)
-
-    barrier = pltpu.get_barrier_semaphore()
-    for dev in (dev_p, dev_x, dev_d, dev_y):
-        pl.semaphore_signal(barrier, inc=1, device_id=dev, device_id_type=MESH)
-    pl.semaphore_wait(barrier, 4)
 
     def rsl(s):
         return pl.ds(s * rows, rows)
@@ -154,11 +157,13 @@
     def normed(s):
         return wide([ynorm[t, rsl(s), :] for t in range(nt)])
 
-    def qd_copy(s, i):
-        return rcopy(qd_send.at[s, i], qd_recv.at[s, i], qd_ssem.at[s, i], qd_rsem.at[s, i], dev_p)
-
-    def qx_copy(s):
-        return rcopy(qx_send.at[s], qx_recv.at[s], qx_ssem.at[s], qx_rsem.at[s], dev_x)
+    def qd_copy(s, i, m):
+        src, dst = ((qd_send, qd_recv), (kd_send, kd_recv))[m]
+        return rcopy(src.at[s, i], dst.at[s, i], qd_ssem.at[s, i, m], qd_rsem.at[s, i, m], dev_p)
+
+    def qx_copy(s, m):
+        src, dst = ((qx_send, qx_recv), (kx_send, kx_recv))[m]
+        return rcopy(src.at[s], dst.at[s], qx_ssem.at[s, m], qx_rsem.at[s, m], dev_x)
 
     def qkv_part(s, i):
         target = 1 - chip if i == 0 else chip
@@ -166,13 +171,21 @@
         for m in range(3):
             low, high = res[:, 2 * m * hw:(2 * m + 1) * hw], res[:, (2 * m + 1) * hw:(2 * m + 2) * hw]
             q_mine[s, i, :, m * hw:(m + 1) * hw] = jnp.where(core == 0, low, high)
-            qd_send[s, i, :, m * hw:(m + 1) * hw] = jnp.where(core == 0, high, low).astype(BF16)
-        qd_copy(s, i).start()
+            away = jnp.where(core == 0, high, low).astype(BF16)
+            if m == 0:
+                qd_send[s, i] = away
+            else:
+                kd_send[s, i, :, (m - 1) * hw:m * hw] = away
+        qd_copy(s, i, 0).start()
+        qd_copy(s, i, 1).start()
 
     def qkv_forward(s):
-        qd_copy(s, 0).wait()
-        qx_send[s] = (q_mine[s, 0] + qd_recv[s, 0].astype(F32)).astype(BF16)
-        qx_copy(s).start()
+        qd_copy(s, 0, 0).wait()
+        qx_send[s] = (q_mine[s, 0, :, 0:hw] + qd_recv[s, 0].astype(F32)).astype(BF16)
+        qx_copy(s, 0).start()
+        qd_copy(s, 0, 1).wait()
+        kx_send[s] = (q_mine[s, 0, :, hw:3 * hw] + kd_recv[s, 0].astype(F32)).astype(BF16)
+        qx_copy(s, 1).start()
 
     def own_bias(b_ref, layer):
         b = b_ref[layer:layer + 1, :].astype(F32)
@@ -189,21 +202,23 @@
         lane = lax.broadcasted_iota(jnp.int32, (n, hw), 1)
         return (lane >= row * hd) & (lane < row * hd + hd)
 
-    def qkv_finish(s, layer):
-        qd_copy(s, 1).wait()
-        qx_copy(s).wait()
-        tot = (q_mine[s, 1] + qd_recv[s, 1].astype(F32)) + qx_recv[s].astype(F32)
-        q = ((tot[:, 0:hw] + own_bias(bq_ref, layer)) * (hd ** -0.5)).astype(BF16)
-        k = (tot[:, hw:2 * hw] + own_bias(bk_ref, layer)).astype(BF16)
-        v = (tot[:, 2 * hw:3 * hw] + own_bias(bv_ref, layer)).astype(BF16)
+    def q_finish(s, layer):
+        qd_copy(s, 1, 0).wait()
+        qx_copy(s, 0).wait()
+        tot = (q_mine[s, 1, :, 0:hw] + qd_recv[s, 1].astype(F32)) + qx_recv[s].astype(F32)
+        q = ((tot + own_bias(bq_ref, layer)) * (hd ** -0.5)).astype(BF16)
+        qblk[...] = jnp.where(head_mask(heads * rows), jnp.dot(expand_mat(), q, preferred_element_type=F32), 0.0).astype(BF16)
+
+    def kv_finish(s, layer):
+        qd_copy(s, 1, 1).wait()
+        qx_copy(s, 1).wait()
+        tot = (q_mine[s, 1, :, hw:3 * hw] + kd_recv[s, 1].astype(F32)) + kx_recv[s].astype(F32)
+        k = (tot[:, 0:hw] + own_bias(bk_ref, layer)).astype(BF16)
+        v = (tot[:, hw:2 * hw] + own_bias(bv_ref, layer)).astype(BF16)
         kfull[rsl(s), :hw] = k.astype(F32)
         vfull[rsl(s), :hw] = v.astype(F32)
-        ex = expand_mat()
-        hm = head_mask(heads * rows)
-        qe = jnp.where(hm, jnp.dot(ex, q, preferred_element_type=F32), 0.0)
-        ke = jnp.dot(ex, k, preferred_element_type=F32)
-        qblk[...] = qe.astype(BF16)
-        snew[...] = jnp.broadcast_to(jnp.sum(qe * ke, axis=1, keepdims=True), snew.shape)
+        ke = jnp.dot(expand_mat(), k, preferred_element_type=F32)
+        snew[...] = jnp.broadcast_to(jnp.sum(qblk[...].astype(F32) * ke, axis=1, keepdims=True), snew.shape)
 
     nr = CB * heads
     per = 128 // nr
@@ -294,8 +309,11 @@
         if lo == 0:
             kv_wait(base, 0)
             kv_wait(base + 1, 0)
-            pa = softmax_of(s, 0, scores_of(base, 0))
-            sbuf[...] = scores_of(base, 1)
+            first = scores_of(base, 0)
+            second = scores_of(base, 1)
+            kv_finish(s, layer)
+            pa = softmax_of(s, 0, first)
+            sbuf[...] = second
             keep_probs(0, *pa)
             refill(base, 0)
             refill(base + 1, 0)
@@ -312,45 +330,43 @@
         if hi == nchunk:
             attention_pair(s, layer, nchunk - 2, True)
 
-    def att_copy(s, i):
-        src, dev = ((0, dev_p), (0, dev_x), (2, dev_p))[i]
-        return rcopy(att.at[s, src], att.at[s, i + 1], at_ssem.at[s, i], at_rsem.at[s, i], dev)
-
-    def att_send(s):
-        hr = heads * rows
-        sel = (lax.broadcasted_iota(jnp.int32, (rows, hr), 1) // heads
-               == lax.broadcasted_iota(jnp.int32, (rows, hr), 0)).astype(F32).astype(BF16)
-        pe = jnp.where(head_mask(hr), jnp.broadcast_to(pnew[:, 0:1], (hr, hw)), 0.0).astype(BF16)
-        o = jnp.dot(sel, pe, preferred_element_type=F32) * vfull[rsl(s), :hw]
-        feat = lax.broadcasted_iota(jnp.int32, (hw, 128), 0)
-        lane = lax.rem(lax.broadcasted_iota(jnp.int32, (hw, 128), 1), heads)
-        own = (feat >= lane * hd) & (feat < lane * hd + hd)
-        for half in range(hr // 128):
-            t = jnp.where(own, tmix[half], 0.0)
-            high = t.astype(BF16)
-            low = (t - high.astype(F32)).astype(BF16)
-            pick = sel[:, half * 128:(half + 1) * 128]
-            for part in (high, low):
-                o = o + lax.dot_general(pick, part, (((1,), (1,)), ((), ())), preferred_element_type=F32)
-        att[s, 0] = o.astype(BF16)
-        att_copy(s, 1).start()
-        att_copy(s, 0).start()
-
-    def att_relay(s):
-        att_copy(s, 1).wait_recv()
-        att_copy(s, 2).start()
+    hrow = LANES // heads
+
+    def att_copies(s, half):
+        return [rcopy(att.at[s, 0, half], att.at[s, i + 1, half], at_ssem.at[s, i, half], at_rsem.at[s, i, half], dev)
+                for i, dev in enumerate((dev_p, dev_x, dev_d))]
+
+    def att_send(s, half):
+        sel = (lax.broadcasted_iota(jnp.int32, (hrow, LANES), 1) // heads
+               == lax.broadcasted_iota(jnp.int32, (hrow, LANES), 0)).astype(F32).astype(BF16)
+        fresh = jnp.broadcast_to(pnew[half * LANES:(half + 1) * LANES, 0:1], (LANES, hw))
+        pe = jnp.where(head_mask(LANES), fresh, 0.0).astype(BF16)
+        first = s * rows + half * hrow
+        o = jnp.dot(sel, pe, preferred_element_type=F32) * vfull[first:first + hrow, :hw]
+        feat = lax.broadcasted_iota(jnp.int32, (hw, LANES), 0)
+        lane = lax.rem(lax.broadcasted_iota(jnp.int32, (hw, LANES), 1), heads)
+        t = jnp.where((feat >= lane * hd) & (feat < lane * hd + hd), tmix[half], 0.0)
+        high = t.astype(BF16)
+        low = (t - high.astype(F32)).astype(BF16)
+        for part in (high, low):
+            o = o + lax.dot_general(sel, part, (((1,), (1,)), ((), ())), preferred_element_type=F32)
+        att[s, 0, half] = o.astype(BF16)
+        p, x, d = att_copies(s, half)
+        x.start()
+        d.start()
+        p.start()
 
     def y_copy(s, which):
         return rcopy(ysend.at[which, s], yrecv.at[which, s], y_ssem.at[which, s], y_rsem.at[which, s], dev_y)
 
     def out_proj(s):
-        att_copy(s, 0).wait()
-        att_copy(s, 1).wait_send()
-        att_copy(s, 2).wait()
+        for half in range(rows // hrow):
+            for cp in att_copies(s, half):
+                cp.wait()
         res = None
         for i, owner in enumerate((r, partner, xpeer, diag)):
             off = pl.multiple_of(owner * hw, 16)
-            t = jnp.dot(att[s, i], wide([wo[n, pl.ds(off, hw), :] for n in range(nt)]), preferred_element_type=F32)
+            t = jnp.dot(jnp.concatenate([att[s, i, h] for h in range(rows // hrow)], axis=0), wide([wo[n, pl.ds(off, hw), :] for n in range(nt)]), preferred_element_type=F32)
             res = t if res is None else res + t
         ysend[0, s] = res.astype(BF16)
         y_copy(s, 0).start()
@@ -373,16 +389,19 @@
     def fc1_part(s):
         yv = normed(s)
 
-        def columns(owner, j):
-            first = owner * (ff_half // LANES) + j * ct
-            return jnp.dot(yv, wide([wf1[first + t] for t in range(ct)]), preferred_element_type=F32)
-
+        def columns(owner, first, n):
+            at = owner * (ff_half // LANES) + first
+            return jnp.dot(yv, wide([wf1[at + t] for t in range(n)]), preferred_element_type=F32)
+
+        tiles = ff_half // LANES
+        res = columns(1 - core, 0, tiles).astype(BF16)
         for j in range(nj):
-            res = columns(1 - core, j).astype(BF16)
             for t in range(ct):
-                fd_send[s, j, t] = res[:, t * LANES:(t + 1) * LANES]
+                fd_send[s, j, t] = res[:, (j * ct + t) * LANES:(j * ct + t + 1) * LANES]
             fd_copy(s, j).start()
-            f_mine[s, j] = columns(core, j)
+        res = columns(core, 0, tiles)
+        for j in range(nj):
+            f_mine[s, j] = res[:, j * CW:(j + 1) * CW]
 
     def fc1_forward(s, lo, hi):
         def body(j, carry):
@@ -454,13 +473,17 @@
             state[rsl(s), :] = new
             stats_send(s, 0, new.astype(F32))
 
+    small[0].wait()
+    pl.semaphore_wait(barrier, 4)
+    stats_send(0, 0, state[rsl(0), :].astype(F32))
+    stats_send(1, 0, state[rsl(1), :].astype(F32))
+    lax.fori_loop(0, RING, prime, 0)
     kfull[...] = jnp.zeros_like(kfull)
     vfull[...] = jnp.zeros_like(vfull)
     pbuf[...] = jnp.zeros_like(pbuf)
     tmix[...] = jnp.zeros_like(tmix)
-    state[...] = hid_ref[...]
-    stats_send(0, 0, state[rsl(0), :].astype(F32))
-    stats_send(1, 0, state[rsl(1), :].astype(F32))
+    for cp in small[1:]:
+        cp.wait()
     w_wait("qkv", 0)
     gain_ph(0, 0, 0)
     qkv_part(0, 0)
@@ -474,61 +497,67 @@
     w_start("o", 0)
     w_start("f1", 0)
     w_start("f2", 0)
-    qkv_finish(0, 0)
-    attention(0, 0, 0, nchunk)
-    att_send(0)
+    q_finish(0, 0)
+    attention(0, 0, 0, nchunk // 2)
+    att_send(0, 0)
+    attention(0, 0, nchunk // 2, nchunk)
+    att_send(0, 1)
     q4 = nchunk // 4
     for layer in range(layers):
         last = layer == layers - 1
-        qkv_finish(1, layer)
+        q_finish(1, layer)
         attention(1, layer, 0, q4)
-        att_relay(0)
-        attention(1, layer, q4, 2 * q4)
         w_wait("o", layer)
         out_proj(0)
+        attention(1, layer, q4, 2 * q4)
+        att_send(1, 0)
         attention(1, layer, 2 * q4, 3 * q4)
-        kv_out(layer)
         mid_ph(0, layer)
         attention(1, layer, 3 * q4, nchunk)
-        att_send(1)
+        att_send(1, 1)
+        kv_out(layer)
+        w_wait("f1", layer)
         gain_ph(0, 1, layer)
-        w_wait("f1", layer)
         fc1_part(0)
-        fc1_forward(0, 0, nj)
-        att_relay(1)
+        fc1_forward(0, 0, 3)
+        out_proj(1)
+        w_start("o", layer + 1)
         w_wait("f2", layer)
         mlp(0, layer, 0, 1)
-        out_proj(1)
-        w_start("o", layer + 1)
+        mid_ph(1, layer)
+        fc1_forward(0, 3, nj)
         mlp(0, layer, 1, 3)
-        mid_ph(1, layer)
-        mlp(0, layer, 3, nj)
         gain_ph(1, 1, layer)
         fc1_part(1)
         w_start("f1", layer + 1)
-        fc1_forward(1, 0, 2)
+        fc1_forward(1, 0, 4)
+        mlp(0, layer, 3, nj)
+        mlp(1, layer, 0, 1)
         end_ph(0, layer)
-        fc1_forward(1, 2, nj)
+        fc1_forward(1, 4, nj)
+        mlp(1, layer, 1, 2)
         if not last:
             w_wait("qkv", layer + 1)
             gain_ph(0, 0, layer + 1)
             qkv_part(0, 0)
+            qkv_part(0, 1)
             qkv_forward(0)
-            qkv_part(0, 1)
-        mlp(1, layer, 0, nj)
+        mlp(1, layer, 2, nj)
         w_start("f2", layer + 1)
         if not last:
-            qkv_finish(0, layer + 1)
+            q_finish(0, layer + 1)
             attention(0, layer + 1, 0, q4)
+            attention(0, layer + 1, q4, 2 * q4)
             end_ph(1, layer)
-            attention(0, layer + 1, q4, 2 * q4)
+            att_send(0, 0)
+            attention(0, layer + 1, 2 * q4, 3 * q4)
             gain_ph(1, 0, layer + 1)
             qkv_part(1, 0)
             qkv_part(1, 1)
             w_start("qkv", layer + 2)
             qkv_forward(1)
-            attention(0, layer + 1, 2 * q4, nchunk)
-            att_send(0)
+            attention(0, layer + 1, 3 * q4, nchunk)
+            att_send(0, 1)
         else:
             end_ph(1, layer)
 
@@ -565,7 +594,6 @@
         vt = v_cache.transpose(0, 1, 2, 4, 3).reshape(layers, batch, hw, s_max)
         vm = pl.BlockSpec(memory_space=pltpu.VMEM)
         hb = pl.BlockSpec(memory_space=pl.ANY)
-        sm = pl.BlockSpec(memory_space=pltpu.SMEM)
         hr = heads * rows
         V = pltpu.VMEM
         D = pltpu.SemaphoreType.DMA
@@ -573,20 +601,24 @@
             V((RING, CB, s_max // LANES, hw, LANES), BF16), V((RING, CB, s_max // LANES, hw, LANES), BF16),
             V((2, 3 * nt, dm, LANES), BF16), V((nt, w_o.shape[1], LANES), BF16),
             V((ff // LANES, dm, LANES), BF16), V((nt, ff, LANES), BF16),
+            pltpu.SMEM((batch,), jnp.int32), V((layers, dm), BF16), V((layers, dm), BF16),
+            V(b_q.shape, BF16), V(b_k.shape, BF16), V(b_v.shape, BF16), V(b_o.shape, BF16),
+            V((layers, dm), BF16), V((layers, dm), BF16), V(b_fc1.shape, BF16), V(b_fc2.shape, BF16),
             V((batch, dm), BF16), V((nt, batch, LANES), BF16),
             V((2, STREAMS, 8, 2 * rows), F32), V((2, STREAMS, 3, 8, 2 * rows), F32),
-            V((STREAMS, 2, rows, 3 * hw), BF16), V((STREAMS, 2, rows, 3 * hw), BF16), V((STREAMS, 2, rows, 3 * hw), F32),
-            V((STREAMS, rows, 3 * hw), BF16), V((STREAMS, rows, 3 * hw), BF16),
+            V((STREAMS, 2, rows, hw), BF16), V((STREAMS, 2, rows, hw), BF16), V((STREAMS, 2, rows, 2 * hw), BF16), V((STREAMS, 2, rows, 2 * hw), BF16),
+            V((STREAMS, 2, rows, 3 * hw), F32),
+            V((STREAMS, rows, hw), BF16), V((STREAMS, rows, hw), BF16), V((STREAMS, rows, 2 * hw), BF16), V((STREAMS, rows, 2 * hw), BF16),
             V((hr, hw), BF16), V((hr, 128), F32), V((CB * heads, s_max), F32), V((s_max // LANES, hr, LANES), BF16), V((hr, 128), F32),
             V((hr // 128, hw, 128), F32),
-            V((STREAMS, 4, rows, hw), BF16), V((batch, 384), F32), V((batch, 384), F32),
+            V((STREAMS, 4, hr // LANES, LANES // heads, hw), BF16), V((batch, 384), F32), V((batch, 384), F32),
             V((2, STREAMS, rows, dm), BF16), V((2, STREAMS, rows, dm), BF16), V((STREAMS, rows, dm), F32),
             V((STREAMS, nj, ct, rows, LANES), BF16), V((STREAMS, nj, ct, rows, LANES), BF16), V((STREAMS, nj, rows, CW), F32),
             V((STREAMS, nj, ct, rows, LANES), BF16), V((STREAMS, nj, ct, rows, LANES), BF16),
             V((STREAMS, 2, nj, ct, rows, LANES), BF16),
-            D((2, s_max // LANES, RING)), D((3, 2 * nt)), D((nt,)), D((ff // LANES,)), D((nt,)), D((2, STREAMS, 3)), D((2, STREAMS, 3)),
-            D((STREAMS, 2)), D((STREAMS, 2)), D((STREAMS,)), D((STREAMS,)),
-            D((STREAMS, 3)), D((STREAMS, 3)), D((2, STREAMS)), D((2, STREAMS)),
+            D((12,)), D((2, s_max // LANES, RING)), D((3, 2 * nt)), D((nt,)), D((ff // LANES,)), D((nt,)), D((2, STREAMS, 3)), D((2, STREAMS, 3)),
+            D((STREAMS, 2, 2)), D((STREAMS, 2, 2)), D((STREAMS, 2)), D((STREAMS, 2)),
+            D((STREAMS, 3, hr // LANES)), D((STREAMS, 3, hr // LANES)), D((2, STREAMS)), D((2, STREAMS)),
             D((STREAMS, nj)), D((STREAMS, nj)), D((STREAMS, nj)), D((STREAMS, nj)), D((STREAMS, nj)), D((STREAMS, nj)),
         ]
         out, kn, vn = pl.pallas_call(
@@ -594,7 +626,7 @@
             out_shape=(jax.ShapeDtypeStruct((batch, dm), BF16),
                        jax.ShapeDtypeStruct((layers, hw, batch), BF16),
                        jax.ShapeDtypeStruct((layers, hw, batch), BF16)),
-            in_specs=[vm, sm, hb, hb, vm, vm, hb, vm, hb, vm, hb, vm, hb, vm, vm, vm, hb, vm, hb, vm],
+            in_specs=[hb] * 20,
             out_specs=(vm, vm, vm),
             scratch_shapes=scratch,
             compiler_params=pltpu.CompilerParams(collective_id=0, has_side_effects=True,

time: 120 us -> 108 us (0.900)
  Pallas kernels: 120 us -> 107 us
    pallas_call x1, Pallas kernels: 118 us -> 105 us  [local_step(): pl.pallas_call(functools.partial(fused, (layers, batch, dm, hw, heads, s_...]
where the time goes in v3:
time: 108 us
  Pallas kernels  107 us (99%)
    pallas_call x1, Pallas kernels, local_step(): pl.pallas_call(functools.partial(fused, (layers, batch, dm, hw, heads, s_...  105 us

profile of v3, /device:TPU:0, one launch (start us, length us, event | category | flops | bytes accessed | tf_op | source)
XLA Modules:
  0.0 107.5 jit_solution(3929485611040881995)
XLA Ops:
  0.6 105.0 %shard_map.211 = (bf16[128,640]{1,0:T(8,128)(2,1)}, bf16[2,320,128]{2,1,0:T(8,128)(2,1)}, bf16[2,320,128]{2,1,0:T(8,128)(2,1)}) custom-call(bf16[128,640]{1,0:T(8,128)(2,1)} %hid_hbm.1, s32[128]{0:T(128)} %len_hbm.1, bf16[2,128,320,256]{3,2,1,0:T(8,128)(2,1)} %bitcast.12, bf16[2,128,320,256]{3,2,1,0:T(8,128)(2,1)} %bitcast.13, bf16[2,640]{1,0:T(2,128)(2,1)} %g1_hbm.1, ...), custom_call_target="tpu_custom_call" | custom-call | tf_op jit(solution)/shard_map/pallas_call | solution.py:624
  105.7 1.9 %shard_map.212 = (bf16[128,640]{1,0:T(8,128)(2,1)}, bf16[2,320,128]{2,1,0:T(8,128)(2,1)}, bf16[2,320,128]{2,1,0:T(8,128)(2,1)}) custom-call(bf16[128,640]{1,0:T(8,128)(2,1)} %get-tuple-element.9.a_ref, bf16[2,320,128]{2,1,0:T(8,128)(2,1)} %get-tuple-element.10.b_ref, bf16[2,320,128]{2,1,0:T(8,128)(2,1)} %get-tuple-element.11.c_ref), custom_call_target="tpu_custom_call" | custom-call | tf_op jit(solution)/shard_map/pallas_call | solution.py:636

commit v4 on v3

--- a/solution.py
+++ b/solution.py
@@ -32,7 +32,7 @@
           qblk, snew, sbuf, pbuf, pnew, tmix, att, kfull, vfull,
           ysend, yrecv, acc,
           fd_send, fd_recv, f_mine, fx_send, fx_recv, u_buf,
-          in_sem, kv_sem, wq_sem, wo_sem, f1_sem, f2_sem, st_ssem, st_rsem, qd_ssem, qd_rsem, qx_ssem, qx_rsem,
+          in_sem, kv_sem, w_sem, st_ssem, st_rsem, qd_ssem, qd_rsem, qx_ssem, qx_rsem,
           at_ssem, at_rsem, y_ssem, y_rsem, fd_ssem, fd_rsem, fx_ssem, fx_rsem, u_ssem, u_rsem):
     layers, batch, dm, hw, heads, s_max, ff = dims
     hd = hw // heads
@@ -66,8 +66,7 @@
         first = lax.rem(ci, STREAMS * nchunk) * CB
         slot = lax.rem(ci, RING)
         src, dst = ((k_hbm, kbuf), (v_hbm, vbuf))[i]
-        return [pltpu.make_async_copy(src.at[layer, pl.ds(first, CB), :, pl.ds(h * LANES, LANES)], dst.at[slot, :, h],
-                                      kv_sem.at[i, h, slot]) for h in range(s_max // LANES)]
+        return [pltpu.make_async_copy(src.at[layer, pl.ds(first, CB)], dst.at[slot], kv_sem.at[i, slot])]
 
     def kv_start(ci, i):
         for cp in kv_copies(ci, i):
@@ -77,30 +76,22 @@
         for cp in kv_copies(ci, i):
             cp.wait()
 
-    def w_each(name, layer, act):
-        def run(src, dst, sems, tiles):
-            def body(t, carry):
-                cp = pltpu.make_async_copy(src.at[layer, :, pl.ds(pl.multiple_of(t * LANES, LANES), LANES)], dst(t), sems(t))
-                cp.start() if act else cp.wait()
-                return carry
-            lax.fori_loop(0, tiles, body, 0)
-
+    def w_copies(name, layer):
         if name == "qkv":
-            for i, w in enumerate((wq_hbm, wk_hbm, wv_hbm)):
-                run(w, lambda t, i=i: wqkv.at[t // nt, i * nt + lax.rem(t, nt)], lambda t, i=i: wq_sem.at[i, t], 2 * nt)
-        elif name == "o":
-            run(wo_hbm, lambda t: wo.at[t], lambda t: wo_sem.at[t], nt)
-        elif name == "f1":
-            run(f1_hbm, lambda t: wf1.at[t], lambda t: f1_sem.at[t], ff // LANES)
-        else:
-            run(f2_hbm, lambda t: wf2.at[t], lambda t: f2_sem.at[t], nt)
+            return [pltpu.make_async_copy(w.at[layer, :, pl.ds(t * 2 * hw, 2 * hw)],
+                                          wqkv.at[t, :, pl.ds(i * 2 * hw, 2 * hw)], w_sem.at[3 + t * 3 + i])
+                    for t in range(2) for i, w in enumerate((wq_hbm, wk_hbm, wv_hbm))]
+        src, dst, i = {"o": (wo_hbm, wo, 0), "f1": (f1_hbm, wf1, 1), "f2": (f2_hbm, wf2, 2)}[name]
+        return [pltpu.make_async_copy(src.at[layer], dst, w_sem.at[i])]
 
     def w_start(name, layer):
         if layer < layers:
-            w_each(name, layer, True)
+            for cp in w_copies(name, layer):
+                cp.start()
 
     def w_wait(name, layer):
-        w_each(name, layer, False)
+        for cp in w_copies(name, layer):
+            cp.wait()
 
     small = [pltpu.make_async_copy(a, b, in_sem.at[n]) for n, (a, b) in enumerate((
         (hid_hbm, state), (len_hbm, len_ref), (g1_hbm, g1_ref), (c1_hbm, c1_ref), (bq_hbm, bq_ref), (bk_hbm, bk_ref),
@@ -165,19 +156,23 @@
         src, dst = ((qx_send, qx_recv), (kx_send, kx_recv))[m]
         return rcopy(src.at[s], dst.at[s], qx_ssem.at[s, m], qx_rsem.at[s, m], dev_x)
 
-    def qkv_part(s, i):
+    def qkv_part(first, i, count=1):
         target = 1 - chip if i == 0 else chip
-        res = jnp.dot(normed(s), wide([wqkv[target, t] for t in range(3 * nt)]), preferred_element_type=F32)
-        for m in range(3):
-            low, high = res[:, 2 * m * hw:(2 * m + 1) * hw], res[:, (2 * m + 1) * hw:(2 * m + 2) * hw]
-            q_mine[s, i, :, m * hw:(m + 1) * hw] = jnp.where(core == 0, low, high)
-            away = jnp.where(core == 0, high, low).astype(BF16)
-            if m == 0:
-                qd_send[s, i] = away
-            else:
-                kd_send[s, i, :, (m - 1) * hw:m * hw] = away
-        qd_copy(s, i, 0).start()
-        qd_copy(s, i, 1).start()
+        yv = wide([ynorm[t, pl.ds(first * rows, count * rows), :] for t in range(nt)])
+        every = jnp.dot(yv, wqkv[target], preferred_element_type=F32)
+        for n in range(count):
+            s = first + n
+            res = every[n * rows:(n + 1) * rows]
+            for m in range(3):
+                low, high = res[:, 2 * m * hw:(2 * m + 1) * hw], res[:, (2 * m + 1) * hw:(2 * m + 2) * hw]
+                q_mine[s, i, :, m * hw:(m + 1) * hw] = jnp.where(core == 0, low, high)
+                away = jnp.where(core == 0, high, low).astype(BF16)
+                if m == 0:
+                    qd_send[s, i] = away
+                    qd_copy(s, i, 0).start()
+                else:
+                    kd_send[s, i, :, (m - 1) * hw:m * hw] = away
+            qd_copy(s, i, 1).start()
 
     def qkv_forward(s):
         qd_copy(s, 0, 0).wait()
@@ -234,7 +229,7 @@
         out = []
         for t in range(nr // 16):
             lhs = qblk[pl.ds(pl.multiple_of(at_row(g) + t * 16, 16), 16), :]
-            d = [jnp.dot(lhs, wide([kbuf[slot, t * 4 + i, h] for h in range(s_max // LANES)]), preferred_element_type=F32)
+            d = [jnp.dot(lhs, kbuf[slot, t * 4 + i], preferred_element_type=F32)
                  for i in range(4)]
             out.append(jnp.where(upper, d[0][0:8], d[1][0:8]))
             out.append(jnp.where(upper, d[2][8:16], d[3][8:16]))
@@ -265,8 +260,7 @@
         slot = lax.rem(base + g, RING)
         seq = lax.broadcasted_iota(jnp.int32, (hw, 128), 1) // heads - lax.rem(g, per) * CB
         for b in range(CB):
-            o = lax.dot_general(wide([vbuf[slot, b, h] for h in range(s_max // LANES)]), rhs, (((1,), (1,)), ((), ())),
-                                preferred_element_type=F32)
+            o = lax.dot_general(vbuf[slot, b], rhs, (((1,), (1,)), ((), ())), preferred_element_type=F32)
             new = jnp.where(seq == b, o, new)
         return new
 
@@ -304,19 +298,20 @@
             if not tail:
                 refill(base + g + 2 + k, 0)
 
+    def open_ph(s, layer):
+        base = (layer * STREAMS + s) * nchunk
+        kv_wait(base, 0)
+        kv_wait(base + 1, 0)
+        first = scores_of(base, 0)
+        second = scores_of(base, 1)
+        kv_finish(s, layer)
+        pa = softmax_of(s, 0, first)
+        sbuf[...] = second
+        keep_probs(0, *pa)
+        refill(base, 0)
+        refill(base + 1, 0)
+
     def attention(s, layer, lo, hi):
-        base = (layer * STREAMS + s) * nchunk
-        if lo == 0:
-            kv_wait(base, 0)
-            kv_wait(base + 1, 0)
-            first = scores_of(base, 0)
-            second = scores_of(base, 1)
-            kv_finish(s, layer)
-            pa = softmax_of(s, 0, first)
-            sbuf[...] = second
-            keep_probs(0, *pa)
-            refill(base, 0)
-            refill(base + 1, 0)
 
         def body(p, carry):
             attention_pair(s, layer, 2 * p, False)
@@ -333,7 +328,7 @@
     hrow = LANES // heads
 
     def att_copies(s, half):
-        return [rcopy(att.at[s, 0, half], att.at[s, i + 1, half], at_ssem.at[s, i, half], at_rsem.at[s, i, half], dev)
+        return [rcopy(att.at[s, r, half], att.at[s, r, half], at_ssem.at[s, i, half], at_rsem.at[s, i, half], dev)
                 for i, dev in enumerate((dev_p, dev_x, dev_d))]
 
     def att_send(s, half):
@@ -350,7 +345,7 @@
         low = (t - high.astype(F32)).astype(BF16)
         for part in (high, low):
             o = o + lax.dot_general(sel, part, (((1,), (1,)), ((), ())), preferred_element_type=F32)
-        att[s, 0, half] = o.astype(BF16)
+        att[s, r, half] = o.astype(BF16)
         p, x, d = att_copies(s, half)
         x.start()
         d.start()
@@ -363,11 +358,8 @@
         for half in range(rows // hrow):
             for cp in att_copies(s, half):
                 cp.wait()
-        res = None
-        for i, owner in enumerate((r, partner, xpeer, diag)):
-            off = pl.multiple_of(owner * hw, 16)
-            t = jnp.dot(jnp.concatenate([att[s, i, h] for h in range(rows // hrow)], axis=0), wide([wo[n, pl.ds(off, hw), :] for n in range(nt)]), preferred_element_type=F32)
-            res = t if res is None else res + t
+        every = wide([jnp.concatenate([att[s, i, h] for h in range(rows // hrow)], axis=0) for i in range(4)])
+        res = jnp.dot(every, wo[...], preferred_element_type=F32)
         ysend[0, s] = res.astype(BF16)
         y_copy(s, 0).start()
 
@@ -390,8 +382,8 @@
         yv = normed(s)
 
         def columns(owner, first, n):
-            at = owner * (ff_half // LANES) + first
-            return jnp.dot(yv, wide([wf1[at + t] for t in range(n)]), preferred_element_type=F32)
+            at = pl.multiple_of(owner * ff_half + first * LANES, LANES)
+            return jnp.dot(yv, wf1[:, pl.ds(at, n * LANES)], preferred_element_type=F32)
 
         tiles = ff_half // LANES
         res = columns(1 - core, 0, tiles).astype(BF16)
@@ -413,44 +405,38 @@
 
         lax.fori_loop(lo, hi, body, 0)
 
-    def fc2_add(s, j, owner):
-        off = pl.multiple_of(owner * ff_half + j * CW, 128)
-        u = wide([u_buf[s, owner, j, t] for t in range(ct)])
-        acc[s] += jnp.dot(u, wide([wf2[n, pl.ds(off, CW), :] for n in range(nt)]), preferred_element_type=F32)
-
-    def mlp(s, layer, lo, hi):
-        if lo == 0:
-            acc[s] = jnp.zeros(acc.shape[1:], F32)
-
+    def fc2_dot(s, owner, lo, hi):
+        off = pl.multiple_of(owner * ff_half + lo * CW, LANES)
+        u = wide([u_buf[s, owner, j, t] for j in range(lo, hi) for t in range(ct)])
+        return jnp.dot(u, wf2[pl.ds(off, (hi - lo) * CW), :], preferred_element_type=F32)
+
+    def mlp(s, layer, lo, hi, plo, phi):
         def body(j, carry):
             fx_copy(s, j).wait()
-            off = pl.multiple_of(core * ff_half + j * CW, 128)
+            off = pl.multiple_of(core * ff_half + j * CW, LANES)
             bias = bf1_ref[layer:layer + 1, pl.ds(off, CW)].astype(F32)
             for t in range(ct):
                 u = (fx_send[s, j, t].astype(F32) + fx_recv[s, j, t].astype(F32)) + bias[:, t * LANES:(t + 1) * LANES]
                 u = u.astype(BF16)
                 u_buf[s, core, j, t] = jnp.maximum(u, jnp.zeros_like(u))
             u_copy(s, j, core).start()
-            fc2_add(s, j, core)
-
-            @pl.when(j > 0)
-            def _():
-                u_copy(s, j - 1, 1 - core).wait_recv()
-                fc2_add(s, j - 1, 1 - core)
             return carry
 
         lax.fori_loop(lo, hi, body, 0)
-        if hi == nj:
-            u_copy(s, nj - 1, 1 - core).wait_recv()
-            fc2_add(s, nj - 1, 1 - core)
-
-            def drain(j, carry):
+        add = fc2_dot(s, core, lo, hi)
+        if phi > plo:
+            for j in range(plo, phi):
+                u_copy(s, j, 1 - core).wait_recv()
+            add = add + fc2_dot(s, 1 - core, plo, phi)
+        if lo > 0:
+            add = acc[s] + add
+        if hi < nj:
+            acc[s] = add
+        else:
+            ysend[1, s] = add.astype(BF16)
+            y_copy(s, 1).start()
+            for j in range(nj):
                 u_copy(s, j, core).wait_send()
-                return carry
-
-            lax.fori_loop(0, nj, drain, 0)
-            ysend[1, s] = acc[s].astype(BF16)
-            y_copy(s, 1).start()
 
     def kv_out(layer):
         kt_ref[layer] = kfull[...].T[:hw, :].astype(BF16)
@@ -486,18 +472,17 @@
         cp.wait()
     w_wait("qkv", 0)
     gain_ph(0, 0, 0)
-    qkv_part(0, 0)
     gain_ph(1, 0, 0)
-    qkv_part(1, 0)
+    qkv_part(0, 0, 2)
+    qkv_part(0, 1, 2)
     qkv_forward(0)
-    qkv_part(0, 1)
     qkv_forward(1)
-    qkv_part(1, 1)
     w_start("qkv", 1)
     w_start("o", 0)
     w_start("f1", 0)
     w_start("f2", 0)
     q_finish(0, 0)
+    open_ph(0, 0)
     attention(0, 0, 0, nchunk // 2)
     att_send(0, 0)
     attention(0, 0, nchunk // 2, nchunk)
@@ -505,59 +490,76 @@
     q4 = nchunk // 4
     for layer in range(layers):
         last = layer == layers - 1
+        w_wait("o", layer)
+        if last:
+            out_proj(0)
         q_finish(1, layer)
-        attention(1, layer, 0, q4)
-        w_wait("o", layer)
-        out_proj(0)
+        if last:
+            open_ph(1, layer)
+            attention(1, layer, 0, q4)
+        else:
+            open_ph(1, layer)
+            attention(1, layer, 0, q4)
+            out_proj(0)
         attention(1, layer, q4, 2 * q4)
         att_send(1, 0)
+        if last:
+            mid_ph(0, layer)
         attention(1, layer, 2 * q4, 3 * q4)
-        mid_ph(0, layer)
+        if not last:
+            mid_ph(0, layer)
         attention(1, layer, 3 * q4, nchunk)
         att_send(1, 1)
-        kv_out(layer)
         w_wait("f1", layer)
         gain_ph(0, 1, layer)
         fc1_part(0)
         fc1_forward(0, 0, 3)
         out_proj(1)
         w_start("o", layer + 1)
+        kv_out(layer)
         w_wait("f2", layer)
-        mlp(0, layer, 0, 1)
+        mlp(0, layer, 0, 1, 0, 0)
         mid_ph(1, layer)
         fc1_forward(0, 3, nj)
-        mlp(0, layer, 1, 3)
+        mlp(0, layer, 1, 2, 0, 1)
+        mlp(0, layer, 2, 3, 1, 2)
         gain_ph(1, 1, layer)
         fc1_part(1)
         w_start("f1", layer + 1)
-        fc1_forward(1, 0, 4)
-        mlp(0, layer, 3, nj)
-        mlp(1, layer, 0, 1)
+        fc1_forward(1, 0, nj if last else 4)
+        mlp(0, layer, 3, nj, 2, nj)
+        mlp(1, layer, 0, 1, 0, 0)
         end_ph(0, layer)
-        fc1_forward(1, 4, nj)
-        mlp(1, layer, 1, 2)
+        if not last:
+            fc1_forward(1, 4, nj)
+        mlp(1, layer, 1, 2, 0, 1)
         if not last:
             w_wait("qkv", layer + 1)
             gain_ph(0, 0, layer + 1)
             qkv_part(0, 0)
+            mlp(1, layer, 2, 3, 1, 2)
+            qkv_forward(0)
             qkv_part(0, 1)
-            qkv_forward(0)
-        mlp(1, layer, 2, nj)
+        else:
+            mlp(1, layer, 2, 3, 1, 2)
+        mlp(1, layer, 3, nj - 1, 2, 3)
+        mlp(1, layer, nj - 1, nj, 3, nj)
         w_start("f2", layer + 1)
         if not last:
             q_finish(0, layer + 1)
+            open_ph(0, layer + 1)
             attention(0, layer + 1, 0, q4)
+            end_ph(1, layer)
             attention(0, layer + 1, q4, 2 * q4)
-            end_ph(1, layer)
             att_send(0, 0)
             attention(0, layer + 1, 2 * q4, 3 * q4)
             gain_ph(1, 0, layer + 1)
             qkv_part(1, 0)
+            attention(0, layer + 1, 3 * q4, nchunk)
+            att_send(0, 1)
+            qkv_forward(1)
             qkv_part(1, 1)
             w_start("qkv", layer + 2)
-            qkv_forward(1)
-            attention(0, layer + 1, 3 * q4, nchunk)
-            att_send(0, 1)
         else:
             end_ph(1, layer)
 
@@ -598,9 +600,8 @@
         V = pltpu.VMEM
         D = pltpu.SemaphoreType.DMA
         scratch = [
-            V((RING, CB, s_max // LANES, hw, LANES), BF16), V((RING, CB, s_max // LANES, hw, LANES), BF16),
-            V((2, 3 * nt, dm, LANES), BF16), V((nt, w_o.shape[1], LANES), BF16),
-            V((ff // LANES, dm, LANES), BF16), V((nt, ff, LANES), BF16),
+            V((RING, CB, hw, s_max), BF16), V((RING, CB, hw, s_max), BF16),
+            V((2, dm, 6 * hw), BF16), V(w_o.shape[1:], BF16), V(w_fc1.shape[1:], BF16), V(w_fc2.shape[1:], BF16),
             pltpu.SMEM((batch,), jnp.int32), V((layers, dm), BF16), V((layers, dm), BF16),
             V(b_q.shape, BF16), V(b_k.shape, BF16), V(b_v.shape, BF16), V(b_o.shape, BF16),
             V((layers, dm), BF16), V((layers, dm), BF16), V(b_fc1.shape, BF16), V(b_fc2.shape, BF16),
@@ -616,7 +617,7 @@
             V((STREAMS, nj, ct, rows, LANES), BF16), V((STREAMS, nj, ct, rows, LANES), BF16), V((STREAMS, nj, rows, CW), F32),
             V((STREAMS, nj, ct, rows, LANES), BF16), V((STREAMS, nj, ct, rows, LANES), BF16),
             V((STREAMS, 2, nj, ct, rows, LANES), BF16),
-            D((12,)), D((2, s_max // LANES, RING)), D((3, 2 * nt)), D((nt,)), D((ff // LANES,)), D((nt,)), D((2, STREAMS, 3)), D((2, STREAMS, 3)),
+            D((12,)), D((2, RING)), D((9,)), D((2, STREAMS, 3)), D((2, STREAMS, 3)),
             D((STREAMS, 2, 2)), D((STREAMS, 2, 2)), D((STREAMS, 2)), D((STREAMS, 2)),
             D((STREAMS, 3, hr // LANES)), D((STREAMS, 3, hr // LANES)), D((2, STREAMS)), D((2, STREAMS)),
             D((STREAMS, nj)), D((STREAMS, nj)), D((STREAMS, nj)), D((STREAMS, nj)), D((STREAMS, nj)), D((STREAMS, nj)),

time: 108 us -> 104 us (0.963)
  Pallas kernels: 107 us -> 103 us
    pallas_call x1, Pallas kernels: 105 us -> 101 us  [local_step(): pl.pallas_call(functools.partial(fused, (layers, batch, dm, hw, heads, s_...]
where the time goes in v4:
time: 104 us
  Pallas kernels  103 us (99%)
    pallas_call x1, Pallas kernels, local_step(): pl.pallas_call(functools.partial(fused, (layers, batch, dm, hw, heads, s_...  101 us

profile of v4, /device:TPU:0, one launch (start us, length us, event | category | flops | bytes accessed | tf_op | source)
XLA Modules:
  0.0 103.6 jit_solution(4146385735058492501)
XLA Ops:
  0.6 101.1 %shard_map.211 = (bf16[128,640]{1,0:T(8,128)(2,1)}, bf16[2,320,128]{2,1,0:T(8,128)(2,1)}, bf16[2,320,128]{2,1,0:T(8,128)(2,1)}) custom-call(bf16[128,640]{1,0:T(8,128)(2,1)} %hid_hbm.1, s32[128]{0:T(128)} %len_hbm.1, bf16[2,128,320,256]{3,2,1,0:T(8,128)(2,1)} %bitcast.12, bf16[2,128,320,256]{3,2,1,0:T(8,128)(2,1)} %bitcast.13, bf16[2,640]{1,0:T(2,128)(2,1)} %g1_hbm.1, ...), custom_call_target="tpu_custom_call" | custom-call | tf_op jit(solution)/shard_map/pallas_call | solution.py:625
  101.8 1.9 %shard_map.212 = (bf16[128,640]{1,0:T(8,128)(2,1)}, bf16[2,320,128]{2,1,0:T(8,128)(2,1)}, bf16[2,320,128]{2,1,0:T(8,128)(2,1)}) custom-call(bf16[128,640]{1,0:T(8,128)(2,1)} %get-tuple-element.9.a_ref, bf16[2,320,128]{2,1,0:T(8,128)(2,1)} %get-tuple-element.10.b_ref, bf16[2,320,128]{2,1,0:T(8,128)(2,1)} %get-tuple-element.11.c_ref), custom_call_target="tpu_custom_call" | custom-call | tf_op jit(solution)/shard_map/pallas_call | solution.py:637

commit v5 on v4

--- a/solution.py
+++ b/solution.py
@@ -11,7 +11,7 @@
 F32 = jnp.float32
 BF16 = jnp.bfloat16
 STREAMS = 2
-RING = 12
+RING = 10
 CB = 8
 CW = 512
 MESH = pl.DeviceIdType.MESH
@@ -459,10 +459,11 @@
             state[rsl(s), :] = new
             stats_send(s, 0, new.astype(F32))
 
+    one, two = range(STREAMS)
     small[0].wait()
     pl.semaphore_wait(barrier, 4)
-    stats_send(0, 0, state[rsl(0), :].astype(F32))
-    stats_send(1, 0, state[rsl(1), :].astype(F32))
+    stats_send(one, 0, state[rsl(one), :].astype(F32))
+    stats_send(two, 0, state[rsl(two), :].astype(F32))
     lax.fori_loop(0, RING, prime, 0)
     kfull[...] = jnp.zeros_like(kfull)
     vfull[...] = jnp.zeros_like(vfull)
@@ -471,103 +472,106 @@
     for cp in small[1:]:
         cp.wait()
     w_wait("qkv", 0)
-    gain_ph(0, 0, 0)
-    gain_ph(1, 0, 0)
-    qkv_part(0, 0, 2)
-    qkv_part(0, 1, 2)
-    qkv_forward(0)
-    qkv_forward(1)
+    gain_ph(one, 0, 0)
+    gain_ph(two, 0, 0)
+    qkv_part(one, 0, 2)
+    qkv_part(one, 1, 2)
+    qkv_forward(one)
+    qkv_forward(two)
     w_start("qkv", 1)
     w_start("o", 0)
     w_start("f1", 0)
     w_start("f2", 0)
-    q_finish(0, 0)
-    open_ph(0, 0)
-    attention(0, 0, 0, nchunk // 2)
-    att_send(0, 0)
-    attention(0, 0, nchunk // 2, nchunk)
-    att_send(0, 1)
+    q_finish(one, 0)
+    open_ph(one, 0)
+    attention(one, 0, 0, nchunk // 2)
+    att_send(one, 0)
+    attention(one, 0, nchunk // 2, nchunk)
+    att_send(one, 1)
     q4 = nchunk // 4
     for layer in range(layers):
         last = layer == layers - 1
         w_wait("o", layer)
         if last:
-            out_proj(0)
-        q_finish(1, layer)
+            out_proj(one)
+        q_finish(two, layer)
         if last:
-            open_ph(1, layer)
-            attention(1, layer, 0, q4)
+            open_ph(two, layer)
+            attention(two, layer, 0, q4)
         else:
-            open_ph(1, layer)
-            attention(1, layer, 0, q4)
-            out_proj(0)
-        attention(1, layer, q4, 2 * q4)
-        att_send(1, 0)
+            open_ph(two, layer)
+            attention(two, layer, 0, q4)
+            out_proj(one)
+        attention(two, layer, q4, 2 * q4)
         if last:
-            mid_ph(0, layer)
-        attention(1, layer, 2 * q4, 3 * q4)
+            mid_ph(one, layer)
+        att_send(two, 0)
+        attention(two, layer, 2 * q4, 3 * q4)
         if not last:
-            mid_ph(0, layer)
-        attention(1, layer, 3 * q4, nchunk)
-        att_send(1, 1)
+            mid_ph(one, layer)
+        attention(two, layer, 3 * q4, nchunk)
+        att_send(two, 1)
         w_wait("f1", layer)
-        gain_ph(0, 1, layer)
-        fc1_part(0)
-        fc1_forward(0, 0, 3)
-        out_proj(1)
+        gain_ph(one, 1, layer)
+        fc1_part(one)
+        fc1_forward(one, 0, 3)
+        out_proj(two)
         w_start("o", layer + 1)
         kv_out(layer)
         w_wait("f2", layer)
-        mlp(0, layer, 0, 1, 0, 0)
-        mid_ph(1, layer)
-        fc1_forward(0, 3, nj)
-        mlp(0, layer, 1, 2, 0, 1)
-        mlp(0, layer, 2, 3, 1, 2)
-        gain_ph(1, 1, layer)
-        fc1_part(1)
+        mlp(one, layer, 0, 1, 0, 0)
+        mid_ph(two, layer)
+        fc1_forward(one, 3, nj)
+        mlp(one, layer, 1, 2, 0, 1)
+        mlp(one, layer, 2, 3, 1, 2)
+        gain_ph(two, 1, layer)
+        fc1_part(two)
         w_start("f1", layer + 1)
-        fc1_forward(1, 0, nj if last else 4)
-        mlp(0, layer, 3, nj, 2, nj)
-        mlp(1, layer, 0, 1, 0, 0)
-        end_ph(0, layer)
+        fc1_forward(two, 0, nj if last else 4)
+        mlp(one, layer, 3, nj, 2, nj)
+        mlp(two, layer, 0, 1, 0, 0)
+        end_ph(one, layer)
         if not last:
-            fc1_forward(1, 4, nj)
-        mlp(1, layer, 1, 2, 0, 1)
+            fc1_forward(two, 4, nj)
+        mlp(two, layer, 1, 2, 0, 1)
         if not last:
             w_wait("qkv", layer + 1)
-            gain_ph(0, 0, layer + 1)
-            qkv_part(0, 0)
-            mlp(1, layer, 2, 3, 1, 2)
-            qkv_forward(0)
-            qkv_part(0, 1)
+            gain_ph(one, 0, layer + 1)
+            qkv_part(one, 0)
+            mlp(two, layer, 2, 3, 1, 2)
+            qkv_forward(one)
+            qkv_part(one, 1)
         else:
-            mlp(1, layer, 2, 3, 1, 2)
-        mlp(1, layer, 3, nj - 1, 2, 3)
-        mlp(1, layer, nj - 1, nj, 3, nj)
+            mlp(two, layer, 2, 3, 1, 2)
+        mlp(two, layer, 3, nj - 1, 2, 3)
+        mlp(two, layer, nj - 1, nj, 3, nj)
         w_start("f2", layer + 1)
         if not last:
-            q_finish(0, layer + 1)
-            open_ph(0, layer + 1)
-            attention(0, layer + 1, 0, q4)
-            end_ph(1, layer)
-            attention(0, layer + 1, q4, 2 * q4)
-            att_send(0, 0)
-            attention(0, layer + 1, 2 * q4, 3 * q4)
-            gain_ph(1, 0, layer + 1)
-            qkv_part(1, 0)
-            attention(0, layer + 1, 3 * q4, nchunk)
-            att_send(0, 1)
-            qkv_forward(1)
-            qkv_part(1, 1)
+            q_finish(one, layer + 1)
+            open_ph(one, layer + 1)
+            attention(one, layer + 1, 0, q4)
+            end_ph(two, layer)
+            attention(one, layer + 1, q4, 2 * q4)
+            att_send(one, 0)
+            attention(one, layer + 1, 2 * q4, 3 * q4)
+            gain_ph(two, 0, layer + 1)
+            qkv_part(two, 0)
+            attention(one, layer + 1, 3 * q4, nchunk)
+            att_send(one, 1)
+            qkv_forward(two)
+            qkv_part(two, 1)
             w_start("qkv", layer + 2)
         else:
-            end_ph(1, layer)
-
-
-def finish(a_ref, b_ref, c_ref, x_ref, y_ref, z_ref):
-    x_ref[...] = a_ref[...]
-    y_ref[...] = b_ref[...]
-    z_ref[...] = c_ref[...]
+            end_ph(two, layer)
+
+
+def finish(a_ref, b_ref, c_ref, x_ref, y_ref, z_ref, sem):
+    copies = [pltpu.make_async_copy(a, b, sem.at[n])
+              for n, (a, b) in enumerate(((a_ref, x_ref), (b_ref, y_ref), (c_ref, z_ref)))]
+    for cp in copies:
+        cp.start()
+    for cp in copies:
+        cp.wait()
 
 
 def solution(mesh):
@@ -624,19 +628,18 @@
         ]
         out, kn, vn = pl.pallas_call(
             functools.partial(fused, (layers, batch, dm, hw, heads, s_max, ff)),
-            out_shape=(jax.ShapeDtypeStruct((batch, dm), BF16),
-                       jax.ShapeDtypeStruct((layers, hw, batch), BF16),
-                       jax.ShapeDtypeStruct((layers, hw, batch), BF16)),
+            out_shape=(V((batch, dm), BF16), V((layers, hw, batch), BF16), V((layers, hw, batch), BF16)),
             in_specs=[hb] * 20,
             out_specs=(vm, vm, vm),
             scratch_shapes=scratch,
             compiler_params=pltpu.CompilerParams(collective_id=0, has_side_effects=True,
-                                                 vmem_limit_bytes=67043328),
+                                                 vmem_limit_bytes=60000000),
         )(hidden, cache_len, kt, vt, ln1_g, ln1_b, w_q, b_q, w_k, b_k, w_v, b_v,
           w_o, b_o, ln2_g, ln2_b, w_fc1, b_fc1, w_fc2, b_fc2)
         out, kn, vn = pl.pallas_call(
             finish, out_shape=tuple(jax.ShapeDtypeStruct(a.shape, a.dtype) for a in (out, kn, vn)),
-            in_specs=[vm] * 3, out_specs=(vm,) * 3)(out, kn, vn)
+            in_specs=[vm] * 3, out_specs=(hb,) * 3, scratch_shapes=[D((3,))],
+            compiler_params=pltpu.CompilerParams(vmem_limit_bytes=4 << 20))(*(pltpu.with_memory_space_constraint(a, pltpu.VMEM) for a in (out, kn, vn)))
         kn = kn.reshape(layers, heads, hd, batch).transpose(0, 3, 1, 2)
         vn = vn.reshape(layers, heads, hd, batch).transpose(0, 3, 1, 2)
         return out, kn, vn

time: 104 us -> 102 us (0.981)
  Pallas kernels: 103 us -> 101 us
    pallas_call x1, Pallas kernels: 1.86 us -> 0.8 us  [local_step(): pl.pallas_call(finish, out_shape=tuple((jax.ShapeDtypeStruct(a.shape, a.d...]
where the time goes in v5:
time: 102 us
  Pallas kernels  101 us (99%)
    pallas_call x1, Pallas kernels, local_step(): pl.pallas_call(functools.partial(fused, (layers, batch, dm, hw, heads, s_...  100 us

profile of v5, /device:TPU:0, one launch (start us, length us, event | category | flops | bytes accessed | tf_op | source)
XLA Modules:
  0.0 102.1 jit_solution(3122492016925829024)
XLA Ops:
  0.6 100.5 %shard_map.211 = (bf16[128,640]{1,0:T(8,128)(2,1)S(1)}, bf16[2,320,128]{2,1,0:T(8,128)(2,1)S(1)}, bf16[2,320,128]{2,1,0:T(8,128)(2,1)S(1)}) custom-call(bf16[128,640]{1,0:T(8,128)(2,1)} %hid_hbm.1, s32[128]{0:T(128)} %len_hbm.1, bf16[2,128,320,256]{3,2,1,0:T(8,128)(2,1)} %bitcast.12, bf16[2,128,320,256]{3,2,1,0:T(8,128)(2,1)} %bitcast.13, ...), custom_call_target="tpu_custom_call" | custom-call | tf_op jit(solution)/shard_map/pallas_call | solution.py:629
  101.1 0.8 shard_map.212

commit v6 on v5

--- a/solution.py
+++ b/solution.py
@@ -422,6 +422,10 @@
             u_copy(s, j, core).start()
             return carry
 
+        if hi == nj and hi - lo == 1:
+            u_copy(s, plo, 1 - core).wait_recv()
+            acc[s] += fc2_dot(s, 1 - core, plo, plo + 1)
+            plo = plo + 1
         lax.fori_loop(lo, hi, body, 0)
         add = fc2_dot(s, core, lo, hi)
         if phi > plo:

time: 102 us -> 103 us (level)
    pallas_call x1, Pallas kernels: 100 us -> 102 us  [local_step(): pl.pallas_call(functools.partial(fused, (layers, batch, dm, hw, heads, s_...]
where the time goes in v6:
time: 103 us
  Pallas kernels  102 us (99%)
    pallas_call x1, Pallas kernels, local_step(): pl.pallas_call(functools.partial(fused, (layers, batch, dm, hw, heads, s_...  102 us

profile of v6, /device:TPU:0, one launch (start us, length us, event | category | flops | bytes accessed | tf_op | source)
XLA Modules:
  0.0 103.2 jit_solution(4623552081371294933)
XLA Ops:
  0.6 101.5 %shard_map.211 = (bf16[128,640]{1,0:T(8,128)(2,1)S(1)}, bf16[2,320,128]{2,1,0:T(8,128)(2,1)S(1)}, bf16[2,320,128]{2,1,0:T(8,128)(2,1)S(1)}) custom-call(bf16[128,640]{1,0:T(8,128)(2,1)} %hid_hbm.1, s32[128]{0:T(128)} %len_hbm.1, bf16[2,128,320,256]{3,2,1,0:T(8,128)(2,1)} %bitcast.12, bf16[2,128,320,256]{3,2,1,0:T(8,128)(2,1)} %bitcast.13, ...), custom_call_target="tpu_custom_call" | custom-call | tf_op jit(solution)/shard_map/pallas_call | solution.py:633
  102.2 0.8 shard_map.212
